TPU v7x, 256 devices: a 8x8x2 block of a 8x8x16 slice. The times are simulated.
256 devices in a mesh: groups: 2 (over z), ep: 128 (over y, x, core).
Axes of the slice: x: 8, y: 8, z: 2, core: 2. Of those that a mesh axis runs over, the one named last changes fastest.
The devices are a block of a 8x8x16 slice.
Arguments:
- tokens: bfloat16 [2048, 2880], P(('groups', 'ep')), parts along dimension 0, may hold values from -6 to 6
- norm_gain: float32 [2880], replicated, may hold values from 0.1 to 1.9
- expert_ids: int32 [2048, 4], P(('groups', 'ep')), parts along dimension 0, may hold values from 0 to 63, all different within a row; in each aligned block of 8 rows (0 to 7, 8 to 15, ...) at most 1 rows name the same one
- gate_codes: int32 [2048, 4], P(('groups', 'ep')), parts along dimension 0, may hold values from 1 to 65535
- w_gate: bfloat16 [128, 2880, 720], P('ep'), may hold values from -0.109375 to 0.109375
- w_up: bfloat16 [128, 2880, 720], P('ep'), may hold values from -0.109375 to 0.109375
- w_down: bfloat16 [128, 720, 2880], P('ep'), may hold values from -0.15625 to 0.15625
Outputs:
- updated: bfloat16 [2048, 2880], P(('groups', 'ep')), parts along dimension 0
There are 2 independent parts, one for each index of `groups`. A program takes and returns all parts, laid end to end along the dimension named above; an argument that names none is the same for every part. Nothing has to cross between parts.
Inputs may be any that keep to these rules, and one draw needn't show every extreme that they name: `expert_ids`: each token names 4 different experts. Among the tokens of one device (aligned blocks of 8 rows) no expert is named more than once, and in every draw some expert is named exactly once by some device's tokens.
All inputs are finite; a program needn't handle non-finite values.
Results may differ from a plain program's by a relative error of at most 0.0049.
Values may be sent and summed in bfloat16 or wider, within the bound.
No kernel may reach another device: no remote copies, remote signals or barrier semaphores. Data moves between devices by JAX's collectives and lax.ppermute only.
A program may use at most 64 MiB of HBM per device.

v0:
```python
import jax
import jax.numpy as jnp
from jax import lax
from jax.sharding import PartitionSpec as P

epsilon = 1e-05


def from_partner(array, axis, bit):
    return lax.ppermute(array, axis, [(i, i ^ 1 << bit) for i in range(lax.axis_size(axis))])


def shards(tokens, norm_gain, expert_ids, gate_codes, w_gate, w_up, w_down):
    values = tokens.astype(jnp.float32)
    normed = (
        values * lax.rsqrt(jnp.mean(values * values, axis=1, keepdims=True) + epsilon) * norm_gain
    ).astype(jnp.bfloat16)
    code_values = gate_codes.astype(jnp.float32)
    weights = code_values / jnp.sum(code_values, axis=1, keepdims=True)
    token_count, top_count = expert_ids.shape
    model_width = tokens.shape[1]
    half_width = model_width // 2
    devices = lax.axis_size("ep")
    experts = devices // 2
    capacity = 2 * token_count * top_count // experts
    flat_ids = expert_ids.reshape(-1)
    onehot = (flat_ids[:, None] == jnp.arange(experts, dtype=jnp.int32)[None, :]).astype(jnp.int32)
    earlier = jnp.cumsum(onehot, axis=0) - onehot
    position = jnp.sum(earlier * onehot, axis=1)
    target = flat_ids * capacity + position
    placing = (target[None, :] == jnp.arange(experts * capacity, dtype=jnp.int32)[:, None]).astype(
        jnp.bfloat16
    )
    repeated = jnp.repeat(normed, top_count, axis=0)
    buffer = jnp.dot(placing, repeated, preferred_element_type=jnp.float32).astype(jnp.bfloat16)
    buffer = buffer.reshape(experts, capacity, model_width)
    parity = lax.axis_index("ep") % 2
    outgoing = buffer.reshape(experts, capacity, 2, half_width)
    outgoing = jnp.transpose(outgoing, (0, 2, 1, 3)).reshape(devices, capacity, half_width)
    arrived = lax.all_to_all(outgoing, "ep", split_axis=0, concat_axis=0, tiled=True)
    partner = from_partner(arrived, "ep", 0)
    lower_half = jnp.where(parity == 0, arrived, partner)
    upper_half = jnp.where(parity == 0, partner, arrived)
    arrived = jnp.concatenate([lower_half, upper_half], axis=2)
    sources = arrived.shape[0]
    slot_count = arrived.shape[1]
    token_rows = arrived.reshape(sources * slot_count, model_width)
    gate_out = jnp.dot(token_rows, w_gate[0], preferred_element_type=jnp.float32)
    upward = jnp.dot(token_rows, w_up[0], preferred_element_type=jnp.float32)
    hidden = (jax.nn.silu(gate_out) * upward).astype(jnp.bfloat16)
    partial_out = jnp.dot(hidden, w_down[0], preferred_element_type=jnp.float32).astype(
        jnp.bfloat16
    )
    partial_out = partial_out.reshape(sources, slot_count, model_width)
    blocks = partial_out.reshape(sources, slot_count, 2, half_width)
    own_block = jnp.where(parity == 0, blocks[:, :, 0], blocks[:, :, 1])
    sent_block = jnp.where(parity == 0, blocks[:, :, 1], blocks[:, :, 0])
    other_block = from_partner(sent_block, "ep", 0)
    summed = (own_block.astype(jnp.float32) + other_block.astype(jnp.float32)).astype(jnp.bfloat16)
    returned = lax.all_to_all(summed, "ep", split_axis=0, concat_axis=0, tiled=True)
    returned = returned.reshape(experts, 2, slot_count, half_width)
    results = jnp.transpose(returned, (0, 2, 1, 3)).reshape(experts, slot_count, model_width)
    per_pair = jnp.dot(
        placing.T,
        results.reshape(experts * capacity, model_width),
        preferred_element_type=jnp.float32,
    )
    mixture = jnp.sum(
        per_pair.reshape(token_count, top_count, model_width) * weights[:, :, None], axis=1
    )
    return (values + mixture).astype(jnp.bfloat16)


def solution(mesh):
    return jax.shard_map(
        shards,
        mesh=mesh,
        in_specs=(
            P(("groups", "ep"), None),
            P(),
            P(("groups", "ep"), None),
            P(("groups", "ep"), None),
            P("ep", None, None),
            P("ep", None, None),
            P("ep", None, None),
        ),
        out_specs=P(("groups", "ep"), None),
        check_vma=False,
    )
```

profile of v0, /device:TPU:514, one launch (start us, length us, event | category | flops | bytes accessed | tf_op | source)
XLA Modules:
  0.0 99.5 jit_solution(11099089923835672365)
XLA Ops:
  0.0 0.9 fusion.25
  0.9 0.8 copy.25
  1.7 0.1 reshape.97
  1.8 0.1 fusion.30
  1.9 0.1 reduce_window_sum.11
  1.9 0.2 select_reduce_fusion
  2.1 0.9 fusion.27
  3.0 0.1 broadcast_in_dim.2
  3.1 0.1 reshape.98
  3.1 0.2 convolution_convert_fusion
  3.4 0.6 reshape_transpose_reshape_reshape.4
  4.0 0.5 broadcast.64
  4.5 3.2 %reduce.1 = bf16[128,1440]{1,0:T(8,128)(2,1)S(1)} reduce(bf16[128,1,1440]{2,1,0:T(2,128)(2,1)S(1)} %reshape_transpose_reshape_reshape.4, bf16[]{:T(256)} %broadcast.64), dimensions={1}, to_apply=%reshape_transpose_reshape_reshape.4.reduce_sub_computation | reduce | bytes 737282 | tf_op jit(solution)/shard_map/reshape;transpose;reshape;reshape | solution.py:39
  7.7 0.4 reshape.104
  8.2 42.6 %all_to_all.10 = bf16[128,2,720]{2,1,0:T(2,128)(2,1)S(1)} all-to-all(bf16[128,2,720]{2,1,0:T(2,128)(2,1)S(1)} %reshape.104), channel_id=1, replica_groups=mesh['groups'=2,'ep'=128] {'ep'}, dimensions={0} | all-to-all | bytes 737280 | tf_op jit(solution)/shard_map/all_to_all | solution.py:40
  50.7 0.7 reshape.105
  51.4 1.0 copy.29
  52.4 0.3 collective-permute-start
  52.7 1.6 %collective-permute-done = bf16[128,1,1440]{0,2,1:T(8,128)(2,1)S(1)} collective-permute-done((bf16[128,1,1440]{0,2,1:T(8,128)(2,1)S(1)}, bf16[128,1,1440]{0,2,1:T(8,128)(2,1)S(1)}, u32[]{:S(2)}, u32[]{:S(2)}) %collective-permute-start) | collective-permute-done | bytes 368672 | tf_op jit(solution)/shard_map/ppermute | solution.py:10
  54.4 0.1 broadcast_select_fusion.1
  54.5 3.5 %fusion.4 = f32[128,720]{0,1:T(8,128)S(1)} fusion(bf16[1,2880,720]{1,2,0:T(8,128)(2,1)} %param.11, bf16[128,1,1440]{0,2,1:T(8,128)(2,1)S(1)} %get-tuple-element.6, bf16[128,1,1440]{0,2,1:T(8,128)(2,1)S(1)} %get-tuple-element.5), kind=kOutput, calls=%fused_computation.4 | convolution fusion | flops 532316160 | bytes 5253120 | tf_op jit(solution)/shard_map/dot_general | solution.py:48
  58.0 8.2 %fusion.6 = bf16[128,2880]{0,1:T(8,128)(2,1)S(1)} fusion(bf16[1,720,2880]{2,1,0:T(8,128)(2,1)} %param.13, bf16[1,2880,720]{1,2,0:T(8,128)(2,1)} %param.12, bf16[128,1,1440]{0,2,1:T(8,128)(2,1)S(1)} %get-tuple-element.6, bf16[128,1,1440]{0,2,1:T(8,128)(2,1)S(1)} %get-tuple-element.5, f32[128,720]{0,1:T(8,128)S(1)} %fusion.4), kind=kOutput, calls=%fused_computation.6 | convolution fusion | flops 1064079360 | bytes 10137600 | tf_op jit(solution)/shard_map/dot_general | solution.py:51
  66.2 0.0 copy-start.1
  66.2 0.0 copy-start
  66.3 0.3 collective-permute-start.1
  66.5 1.6 %collective-permute-done.1 = bf16[128,1,1440]{0,2,1:T(8,128)(2,1)S(1)} collective-permute-done((bf16[128,1,1440]{0,2,1:T(8,128)(2,1)S(1)}, bf16[128,1,1440]{0,2,1:T(8,128)(2,1)S(1)}, u32[]{:S(2)}, u32[]{:S(2)}) %collective-permute-start.1) | collective-permute-done | bytes 368672 | tf_op jit(solution)/shard_map/ppermute | solution.py:10
  68.1 0.1 fusion.18
  68.2 0.9 reduce.2
  69.1 0.2 copy.32
  69.3 1.2 %reshape.106 = bf16[128,2,720]{2,1,0:T(2,128)(2,1)} reshape(bf16[128,1440]{1,0:T(8,128)(2,1)S(1)} %copy.32) | data formatting | bytes 737280
  70.5 7.8 %all-to-all-start.1 = ((bf16[128,2,720]{2,1,0:T(2,128)(2,1)}), bf16[128,2,720]{2,1,0:T(2,128)(2,1)S(1)}, u32[]{:S(2)}, u32[]{:S(2)}) async-start(bf16[128,2,720]{2,1,0:T(2,128)(2,1)} %reshape.106), calls=%async_computation.1 | async-start | bytes 786432 | tf_op jit(solution)/shard_map/all_to_all | solution.py:60
  78.3 0.1 reduce_sum.39
  78.4 0.1 copy.26
  78.5 0.0 copy-done.1
  78.5 16.5 %all-to-all-done.1 = bf16[128,2,720]{2,1,0:T(2,128)(2,1)S(1)} async-done(((bf16[128,2,720]{2,1,0:T(2,128)(2,1)}), bf16[128,2,720]{2,1,0:T(2,128)(2,1)S(1)}, u32[]{:S(2)}, u32[]{:S(2)}) %all-to-all-start.1) | async-done | bytes 368672 | tf_op jit(solution)/shard_map/all_to_all | solution.py:60
  95.0 0.7 reshape.107
  95.7 2.6 %reduce = bf16[128,1440]{1,0:T(8,128)(2,1)S(1)} reduce(bf16[128,1,1440]{2,1,0:T(2,128)(2,1)S(1)} %reshape.107, bf16[]{:T(256)} %constant.38), dimensions={1}, to_apply=%all_to_all.7.reduce_sub_computation | reduce | bytes 737282 | tf_op jit(solution)/shard_map/all_to_all | solution.py:60
  98.3 0.3 reshape.101
  98.6 0.3 fusion.15
  98.8 0.0 copy-done
  98.8 0.6 fusion.28
  (6 shorter events, 0.1 us)
Async XLA Ops:
  52.4 2.0 %collective-permute-start = (bf16[128,1,1440]{0,2,1:T(8,128)(2,1)S(1)}, bf16[128,1,1440]{0,2,1:T(8,128)(2,1)S(1)}, u32[]{:S(2)}, u32[]{:S(2)}) collective-permute-start(bf16[128,1,1440]{0,2,1:T(8,128)(2,1)S(1)} %copy.29), channel_id=1, source_target_pairs={{0,1},{1,0},{2,3},{3,2},{4,5},{5,4},{6,7},{7,6},{8,9},{9,8},{10,11... | collective-permute-start | bytes 1105928 | tf_op jit(solution)/shard_map/ppermute | solution.py:10
  66.2 12.3 %copy-start.1 = (s32[8,4]{0,1:T(4,128)S(1)}, s32[8,4]{0,1:T(4,128)}, u32[]{:S(2)}) copy-start(s32[8,4]{0,1:T(4,128)} %param.10) | copy-start | bytes 388
  66.2 32.6 %copy-start = (bf16[8,2880]{1,0:T(8,128)(2,1)S(1)}, bf16[8,2880]{1,0:T(8,128)(2,1)}, u32[]{:S(2)}) copy-start(bf16[8,2880]{1,0:T(8,128)(2,1)} %param.7) | copy-start | bytes 138244
  66.3 1.8 %collective-permute-start.1 = (bf16[128,1,1440]{0,2,1:T(8,128)(2,1)S(1)}, bf16[128,1,1440]{0,2,1:T(8,128)(2,1)S(1)}, u32[]{:S(2)}, u32[]{:S(2)}) collective-permute-start(bf16[128,1,1440]{0,2,1:T(8,128)(2,1)S(1)} %select_bitcast_fusion), channel_id=1, source_target_pairs={{0,1},{1,0},{2,3},{3,2},{4,5},{5,4},{6,7},{7,6},{8,9},{9,8},{10,11... | collective-permute-start | bytes 1105928 | tf_op jit(solution)/shard_map/ppermute | solution.py:10
  70.5 24.5 %all-to-all-start.1 = ((bf16[128,2,720]{2,1,0:T(2,128)(2,1)}), bf16[128,2,720]{2,1,0:T(2,128)(2,1)S(1)}, u32[]{:S(2)}, u32[]{:S(2)}) async-start(bf16[128,2,720]{2,1,0:T(2,128)(2,1)} %reshape.106), calls=%async_computation.1 | async-start | bytes 786432 | tf_op jit(solution)/shard_map/all_to_all | solution.py:60
where the time goes:
time: 101 us; the launch traced here: 99.5 us
  blocking collectives  42.6 us (42%)
  waiting for transfers between devices  19.7 us (20%)
  matrix products  12.2 us (12%)
  other arithmetic  9.73 us (10%)
  starting transfers between devices  8.41 us (8%)
  local copies, waits for them, and re-layouts  6.66 us (7%)
    all_to_all x1, blocking collectives, shards(): lax.all_to_all(outgoing, 'ep', split_axis=0, concat_axis=0, tiled=True)  42.6 us
    all_to_all x1, waiting for transfers between devices, shards(): lax.all_to_all(summed, 'ep', split_axis=0, concat_axis=0, tiled=True)  16.5 us
    dot_general x1, matrix products, shards(): jnp.dot(hidden, w_down[0], preferred_element_type=jnp.float32)  8.21 us
    all_to_all x1, starting transfers between devices, shards(): lax.all_to_all(summed, 'ep', split_axis=0, concat_axis=0, tiled=True)  7.83 us
    unnamed x10, local copies, waits for them, and re-layouts  3.91 us
    dot_general x1, matrix products, shards(): jnp.dot(token_rows, w_gate[0], preferred_element_type=jnp.float32)  3.52 us
    another operation x1, other arithmetic, shards(): jnp.transpose(outgoing, (0, 2, 1, 3)).reshape(devices, capacity, half_width)  3.22 us
    ppermute x2, waiting for transfers between devices, from_partner(): lax.ppermute(array, axis, [(i, i ^ 1 << bit) for i in range(lax.axis_size...  3.2 us
  transfers between devices with their start and end apart: 3, of which 3 were waited for; matrix products, arithmetic and copies ran while one was open for 0% of the time, Pallas kernels for 0%

commit v1 on v0

v1 whole, which is shorter than its diff:
```python
import functools

import jax
import jax.numpy as jnp
from jax import lax
from jax.experimental import pallas as pl
from jax.experimental.pallas import tpu as pltpu
from jax.sharding import PartitionSpec as P

epsilon = 1e-05
PIECES = 8
NT = (((1,), (1,)), ((), ()))


def piece_width(model_width):
    return -(-model_width // (PIECES * 128)) * 128


def stack_pieces(rows, width):
    d = rows.shape[1]
    parts = []
    for s in range(PIECES):
        part = rows[:, s * width : min((s + 1) * width, d)]
        if part.shape[1] < width:
            part = jnp.concatenate(
                [part, jnp.zeros((rows.shape[0], width - part.shape[1]), rows.dtype)], axis=1
            )
        parts.append(part)
    return jnp.concatenate(parts, axis=0)


def swap_matrix(outer, inner):
    total = outer * inner
    row = lax.broadcasted_iota(jnp.int32, (total, total), 0)
    col = lax.broadcasted_iota(jnp.int32, (total, total), 1)
    source = (row % inner) * outer + row // inner
    return jnp.where(col == source, 1.0, 0.0).astype(jnp.bfloat16)


def route_kernel(tokens_ref, gain_ref, ids_ref, out_ref, *, experts, width):
    values = tokens_ref[...].astype(jnp.float32)
    count = values.shape[0]
    scale = lax.rsqrt(jnp.mean(values * values, axis=1, keepdims=True) + epsilon)
    normed = values * scale * gain_ref[...]
    stacked = stack_pieces(normed, width).astype(jnp.bfloat16)
    ids = ids_ref[...].astype(jnp.float32)
    top = ids.shape[0]
    columns = PIECES * count
    spread = jnp.where(
        lax.broadcasted_iota(jnp.int32, (count, columns), 1) % count
        == lax.broadcasted_iota(jnp.int32, (count, columns), 0),
        1.0,
        0.0,
    )
    ids_wide = jnp.dot(
        ids.astype(jnp.bfloat16), spread.astype(jnp.bfloat16), preferred_element_type=jnp.float32
    ).astype(jnp.int32)
    piece = lax.broadcasted_iota(jnp.int32, (top, columns), 1) // count
    wanted = ids_wide * PIECES + piece
    row = lax.broadcasted_iota(jnp.int32, (experts * PIECES, columns), 0)
    hit = row == wanted[0:1, :]
    for k in range(1, top):
        hit = jnp.logical_or(hit, row == wanted[k : k + 1, :])
    placing = jnp.where(hit, 1.0, 0.0).astype(jnp.bfloat16)
    out_ref[...] = jnp.dot(placing, stacked, preferred_element_type=jnp.float32).astype(
        jnp.bfloat16
    )


def expert_kernel(own_ref, other_ref, gate_ref, up_ref, down_ref, own_out, other_out, *, width):
    rows = own_ref.shape[0] // PIECES
    model = gate_ref.shape[1]
    swap = swap_matrix(PIECES, rows)
    halves = []
    for ref in (own_ref, other_ref):
        moved = jnp.dot(swap, ref[...], preferred_element_type=jnp.float32).astype(jnp.bfloat16)
        halves.append(
            jnp.concatenate([moved[s * rows : (s + 1) * rows] for s in range(PIECES)], axis=1)
        )
    x = jnp.concatenate(halves, axis=0)[:, :model]
    gate = lax.dot_general(gate_ref[...], x, NT, preferred_element_type=jnp.float32)
    up = lax.dot_general(up_ref[...], x, NT, preferred_element_type=jnp.float32)
    hidden = (gate * jax.nn.sigmoid(gate) * up).T.astype(jnp.bfloat16)
    out = jnp.dot(hidden, down_ref[...], preferred_element_type=jnp.float32).astype(jnp.bfloat16)
    own_out[...] = out[:rows]
    other_out[...] = out[rows:]


def add_kernel(own_ref, arrived_ref, out_ref, *, width):
    rows = own_ref.shape[0]
    total = own_ref[...].astype(jnp.float32) + arrived_ref[...].astype(jnp.float32)
    stacked = stack_pieces(total, width).astype(jnp.bfloat16)
    out_ref[...] = jnp.dot(
        swap_matrix(rows, PIECES), stacked, preferred_element_type=jnp.float32
    ).astype(jnp.bfloat16)


def combine_kernel(tokens_ref, ids_ref, codes_ref, returned_ref, out_ref, *, width):
    ids = ids_ref[...].T
    codes = codes_ref[...].astype(jnp.float32)
    weights = (codes / jnp.sum(codes, axis=0, keepdims=True)).T
    count, top = ids.shape
    rows = PIECES * count
    slots = returned_ref.shape[0]
    piece = lax.broadcasted_iota(jnp.int32, (rows, 1), 0) // count
    col = lax.broadcasted_iota(jnp.int32, (rows, slots), 1)
    mixture = None
    for k in range(top):
        wanted = jnp.concatenate([ids[:, k : k + 1]] * PIECES, axis=0) * PIECES + piece
        taking = jnp.where(col == wanted, 1.0, 0.0).astype(jnp.bfloat16)
        picked = jnp.dot(taking, returned_ref[...], preferred_element_type=jnp.float32)
        term = picked * jnp.concatenate([weights[:, k : k + 1]] * PIECES, axis=0)
        mixture = term if mixture is None else mixture + term
    model = tokens_ref.shape[1]
    for s in range(PIECES):
        span = min((s + 1) * width, model) - s * width
        here = pl.ds(s * width, span)
        out_ref[:, here] = (
            tokens_ref[:, here].astype(jnp.float32)
            + mixture[s * count : (s + 1) * count, :span]
        ).astype(jnp.bfloat16)


VMEM = pl.BlockSpec(memory_space=pltpu.VMEM)


def call(kernel, out_shape, limit, cost, *args):
    many = isinstance(out_shape, tuple)
    return pl.pallas_call(
        kernel,
        out_shape=out_shape,
        in_specs=[VMEM] * len(args),
        out_specs=(VMEM,) * len(out_shape) if many else VMEM,
        compiler_params=pltpu.CompilerParams(vmem_limit_bytes=limit),
        cost_estimate=pl.CostEstimate(flops=cost, bytes_accessed=0, transcendentals=0),
    )(*args)


def shards(tokens, norm_gain, expert_ids, gate_codes, w_gate, w_up, w_down):
    devices = lax.axis_size("ep")
    experts = devices // 2
    count, model = tokens.shape
    width = piece_width(model)
    slots = experts * PIECES
    message = jax.ShapeDtypeStruct((slots, width), jnp.bfloat16)
    same_core = [[2 * i + c for i in range(experts)] for c in range(2)]
    partner = [(i, i ^ 1) for i in range(devices)]
    ids = expert_ids.T
    codes = gate_codes.T

    def exchange(rows):
        return lax.all_to_all(
            rows.reshape(experts, PIECES, width),
            "ep",
            split_axis=0,
            concat_axis=0,
            axis_index_groups=same_core,
            tiled=True,
        ).reshape(slots, width)

    outgoing = call(
        functools.partial(route_kernel, experts=experts, width=width),
        message,
        4 << 20,
        20_000_000_000,
        tokens,
        norm_gain.reshape(1, model),
        ids,
    )
    arrived = exchange(outgoing)
    other = lax.ppermute(arrived, "ep", partner)
    share = jax.ShapeDtypeStruct((experts, model), jnp.bfloat16)
    own_share, other_share = call(
        functools.partial(expert_kernel, width=width),
        (share, share),
        32 << 20,
        2_000_000_000,
        arrived,
        other,
        w_gate[0].T,
        w_up[0].T,
        w_down[0],
    )
    returned = exchange(
        call(
            functools.partial(add_kernel, width=width),
            message,
            8 << 20,
            1_000_000,
            own_share,
            lax.ppermute(other_share, "ep", partner),
        )
    )
    return call(
        functools.partial(combine_kernel, width=width),
        jax.ShapeDtypeStruct((count, model), jnp.bfloat16),
        8 << 20,
        1_000_000,
        tokens,
        ids,
        codes,
        returned,
    )


def solution(mesh):
    return jax.shard_map(
        shards,
        mesh=mesh,
        in_specs=(
            P(("groups", "ep"), None),
            P(),
            P(("groups", "ep"), None),
            P(("groups", "ep"), None),
            P("ep", None, None),
            P("ep", None, None),
            P("ep", None, None),
        ),
        out_specs=P(("groups", "ep"), None),
        check_vma=False,
    )
```

time: 101 us -> 71.9 us (0.71); the launches traced: 99.5 us -> 71.7 us
  blocking collectives: 42.6 us -> 60.1 us
  waiting for transfers between devices: 19.7 us -> 3.29 us
  matrix products: 12.2 us -> 0 us
  other arithmetic: 9.73 us -> 0 us
  starting transfers between devices: 8.41 us -> 0.26 us
  Pallas kernels: 0 us -> 5.72 us
  local copies, waits for them, and re-layouts: 6.66 us -> 2.21 us
    all_to_all x1 -> x2, blocking collectives: 42.6 us -> 60.1 us  [exchange(): lax.all_to_all(rows.reshape(experts, PIECES, width), 'ep', split_axis=0,...]
    all_to_all x1 -> x0, waiting for transfers between devices: 16.5 us -> none  [shards(): lax.all_to_all(summed, 'ep', split_axis=0, concat_axis=0, tiled=True)]
    dot_general x4 -> x0, matrix products: 12.2 us -> none  [the longest x1 8.21 us: shards(): jnp.dot(hidden, w_down[0], preferred_element_type=jnp.float32)]
    all_to_all x1 -> x0, starting transfers between devices: 7.83 us -> none  [shards(): lax.all_to_all(summed, 'ep', split_axis=0, concat_axis=0, tiled=True)]
    pallas_call x0 -> x4, Pallas kernels: none -> 5.72 us  [call(): pl.pallas_call(kernel, out_shape=out_shape, in_specs=[VMEM] * len(args),...]
    another operation x2 -> x0, other arithmetic: 3.28 us -> none  [the longest x1 3.22 us: shards(): jnp.transpose(outgoing, (0, 2, 1, 3)).reshape(devices, capacity, half_width)]
    convert_element_type x5 -> x0, other arithmetic: 2.63 us -> none  [the longest x2 1.05 us: shards(): (own_block.astype(jnp.float32) + other_block.astype(jnp.float32)).astype(...]
    all_to_all x1 -> x0, other arithmetic: 2.57 us -> none  [shards(): lax.all_to_all(summed, 'ep', split_axis=0, concat_axis=0, tiled=True)]
  transfers between devices with their start and end apart: 3 -> 2, of which waited for: 3 -> 2; matrix products, arithmetic and copies ran while one was open for 0% -> 0% of each run, Pallas kernels for 0% -> 0%
where the time goes in v1:
time: 71.9 us; the launch traced here: 71.7 us
  blocking collectives  60.1 us (84%)
  Pallas kernels  5.72 us (8%)
  waiting for transfers between devices  3.29 us (5%)
  local copies, waits for them, and re-layouts  2.21 us (3%)
    all_to_all x2, blocking collectives, exchange(): lax.all_to_all(rows.reshape(experts, PIECES, width), 'ep', split_axis=0,...  60.1 us
    pallas_call x4, Pallas kernels, call(): pl.pallas_call(kernel, out_shape=out_shape, in_specs=[VMEM] * len(args),...  5.72 us
    ppermute x1, waiting for transfers between devices, shards(): other = lax.ppermute(arrived, 'ep', partner)  1.72 us
    ppermute x1, waiting for transfers between devices, shards(): lax.ppermute(other_share, 'ep', partner)  1.57 us
    unnamed x16, local copies, waits for them, and re-layouts  1.5 us
  transfers between devices with their start and end apart: 2, of which 2 were waited for; matrix products, arithmetic and copies ran while one was open for 0% of the time, Pallas kernels for 0%

profile of v1, /device:TPU:514, one launch (start us, length us, event | category | flops | bytes accessed | tf_op | source)
XLA Modules:
  0.0 71.7 jit_solution(16981413525340555100)
XLA Ops:
  0.0 0.7 reshape.15.gain_ref
  0.7 0.0 copy-start.3
  0.7 0.8 %copy-done.3 = bf16[8,2880]{1,0:T(8,128)(2,1)S(1)} copy-done((bf16[8,2880]{1,0:T(8,128)(2,1)S(1)}, bf16[8,2880]{1,0:T(8,128)(2,1)}, u32[]{:S(2)}) %copy-start.3) | copy-done | bytes 46104
  1.5 0.0 copy-start.5
  1.5 0.7 copy-done.5
  2.2 0.0 copy-start
  2.2 0.0 copy-start.1
  2.2 0.0 copy-start.2
  2.2 0.4 shard_map.73
  2.6 37.9 %all_to_all.10 = bf16[64,8,384]{2,1,0:T(8,128)(2,1)S(1)} all-to-all(bf16[64,8,384]{2,1,0:T(8,128)(2,1)S(1)} %bitcast.20), channel_id=1, replica_groups={{0,2,4,6,8,10,12,14,16,18,20,22,24,26,28,30,32,34,36,38,40,42,44,46,48,..., dimensions={0} | all-to-all | bytes 786432 | tf_op jit(solution)/shard_map/all_to_all | solution.py:152
  40.4 0.0 collective-permute-start
  40.5 1.7 %collective-permute-done.other_ref = bf16[512,384]{1,0:T(8,128)(2,1)S(1)} collective-permute-done((bf16[512,384]{1,0:T(8,128)(2,1)S(1)}, bf16[512,384]{1,0:T(8,128)(2,1)S(1)}, u32[]{:S(2)}, u32[]{:S(2)}) %collective-permute-start) | collective-permute-done | bytes 393248 | tf_op jit(solution)/shard_map/ppermute | solution.py:171
  42.2 0.0 copy-done
  42.2 0.0 copy-done.1
  42.2 0.0 copy-done.2
  42.2 0.0 copy-start.4
  42.2 0.0 copy-start.6
  42.2 0.0 copy-start.7
  42.2 3.8 %shard_map.74 = (bf16[64,2880]{1,0:T(8,128)(2,1)S(1)}, bf16[64,2880]{1,0:T(8,128)(2,1)S(1)}) custom-call(bf16[512,384]{1,0:T(8,128)(2,1)S(1)} %bitcast.17, bf16[512,384]{1,0:T(8,128)(2,1)S(1)} %collective-permute-done.other_ref, bf16[720,2880]{1,0:T(8,128)(2,1)S(1)} %bitcast.13, bf16[720,2880]{1,0:T(8,128)(2,1)S(1)} %bitcast.14, bf16[720,2880]{1,0:T(8,128)(2,1)S(1)} %bitcast.15), custom_call_target="tpu_custom_call" | custom-call | flops 2000000000 | tf_op jit(solution)/shard_map/pallas_call | solution.py:129
  46.0 0.3 collective-permute-start.1
  46.2 1.6 %collective-permute-done.1.arrived_ref = bf16[64,2880]{1,0:T(8,128)(2,1)S(1)} collective-permute-done((bf16[64,2880]{1,0:T(8,128)(2,1)S(1)}, bf16[64,2880]{1,0:T(8,128)(2,1)S(1)}, u32[]{:S(2)}, u32[]{:S(2)}) %collective-permute-start.1) | collective-permute-done | bytes 368672 | tf_op jit(solution)/shard_map/ppermute | solution.py:191
  47.8 0.5 shard_map.75
  48.3 22.2 %all_to_all.11 = bf16[64,8,384]{2,1,0:T(8,128)(2,1)S(1)} all-to-all(bf16[64,8,384]{2,1,0:T(8,128)(2,1)S(1)} %bitcast.18), channel_id=1, replica_groups={{0,2,4,6,8,10,12,14,16,18,20,22,24,26,28,30,32,34,36,38,40,42,44,46,48,..., dimensions={0} | all-to-all | bytes 786432 | tf_op jit(solution)/shard_map/all_to_all | solution.py:152
  70.5 0.0 copy-done.4
  70.5 0.0 copy-done.6
  70.5 0.0 copy-done.7
  70.6 1.1 %shard_map.76 = bf16[8,2880]{1,0:T(8,128)(2,1)} custom-call(bf16[8,2880]{1,0:T(8,128)(2,1)S(1)} %copy-done.4, s32[4,8]{1,0:T(4,128)S(1)} %bitcast.22, s32[4,8]{1,0:T(4,128)S(1)} %bitcast.23, bf16[512,384]{1,0:T(8,128)(2,1)S(1)} %bitcast.19), custom_call_target="tpu_custom_call" | custom-call | flops 1000000 | tf_op jit(solution)/shard_map/pallas_call | solution.py:129
Async XLA Ops:
  0.7 0.8 %copy-start.3 = (bf16[8,2880]{1,0:T(8,128)(2,1)S(1)}, bf16[8,2880]{1,0:T(8,128)(2,1)}, u32[]{:S(2)}) copy-start(bf16[8,2880]{1,0:T(8,128)(2,1)} %tokens_ref.3) | copy-start | bytes 138244
  1.5 0.7 copy-start.5
  2.2 40.0 %copy-start = (bf16[1,2880,720]{1,2,0:T(8,128)(2,1)S(1)}, bf16[1,2880,720]{1,2,0:T(8,128)(2,1)}, u32[]{:S(2)}) copy-start(bf16[1,2880,720]{1,2,0:T(8,128)(2,1)} %param.11) | copy-start | bytes 12441604
  2.2 40.0 %copy-start.1 = (bf16[1,2880,720]{1,2,0:T(8,128)(2,1)S(1)}, bf16[1,2880,720]{1,2,0:T(8,128)(2,1)}, u32[]{:S(2)}) copy-start(bf16[1,2880,720]{1,2,0:T(8,128)(2,1)} %param.12) | copy-start | bytes 12441604
  2.2 40.0 %copy-start.2 = (bf16[1,720,2880]{2,1,0:T(8,128)(2,1)S(1)}, bf16[1,720,2880]{2,1,0:T(8,128)(2,1)}, u32[]{:S(2)}) copy-start(bf16[1,720,2880]{2,1,0:T(8,128)(2,1)} %param.13) | copy-start | bytes 12441604
  40.4 1.7 %collective-permute-start = (bf16[512,384]{1,0:T(8,128)(2,1)S(1)}, bf16[512,384]{1,0:T(8,128)(2,1)S(1)}, u32[]{:S(2)}, u32[]{:S(2)}) collective-permute-start(bf16[512,384]{1,0:T(8,128)(2,1)S(1)} %bitcast.16), channel_id=1, source_target_pairs={{0,1},{1,0},{2,3},{3,2},{4,5},{5,4},{6,7},{7,6},{8,9},{9,8},{10,11... | collective-permute-start | bytes 1179656 | tf_op jit(solution)/shard_map/ppermute | solution.py:171
  42.2 28.4 %copy-start.4 = (bf16[8,2880]{1,0:T(8,128)(2,1)S(1)}, bf16[8,2880]{1,0:T(8,128)(2,1)}, u32[]{:S(2)}) copy-start(bf16[8,2880]{1,0:T(8,128)(2,1)} %tokens_ref.3) | copy-start | bytes 138244
  42.2 28.4 %copy-start.6 = (s32[8,4]{0,1:T(4,128)S(1)}, s32[8,4]{0,1:T(4,128)}, u32[]{:S(2)}) copy-start(s32[8,4]{0,1:T(4,128)} %param.9) | copy-start | bytes 388
  42.2 28.3 %copy-start.7 = (s32[8,4]{0,1:T(4,128)S(1)}, s32[8,4]{0,1:T(4,128)}, u32[]{:S(2)}) copy-start(s32[8,4]{0,1:T(4,128)} %param.10) | copy-start | bytes 388
  46.0 1.8 %collective-permute-start.1 = (bf16[64,2880]{1,0:T(8,128)(2,1)S(1)}, bf16[64,2880]{1,0:T(8,128)(2,1)S(1)}, u32[]{:S(2)}, u32[]{:S(2)}) collective-permute-start(bf16[64,2880]{1,0:T(8,128)(2,1)S(1)} %get-tuple-element.8), channel_id=1, source_target_pairs={{0,1},{1,0},{2,3},{3,2},{4,5},{5,4},{6,7},{7,6},{8,9},{9,8},{10,11... | collective-permute-start | bytes 1105928 | tf_op jit(solution)/shard_map/ppermute | solution.py:191

commit v2 on v1

v2 whole, which is shorter than its diff:
```python
import functools

import jax
import jax.numpy as jnp
from jax import lax
from jax.experimental import pallas as pl
from jax.experimental.pallas import tpu as pltpu
from jax.sharding import PartitionSpec as P

epsilon = 1e-05
PIECES = 8
BLOCK = 32
NT = (((1,), (1,)), ((), ()))
F32 = jnp.float32
BF16 = jnp.bfloat16


def iota(shape, axis):
    return lax.broadcasted_iota(jnp.int32, shape, axis)


def onehot(mask):
    return jnp.where(mask, 1.0, 0.0).astype(BF16)


def matmul(a, b):
    return jnp.dot(a, b, preferred_element_type=F32)


def piece_width(model_width):
    return -(-model_width // (PIECES * 128)) * 128


def stack_pieces(rows, width):
    n, d = rows.shape
    parts = []
    for s in range(PIECES):
        part = rows[:, s * width : min((s + 1) * width, d)]
        if part.shape[1] < width:
            part = jnp.concatenate(
                [part, jnp.zeros((n, width - part.shape[1]), rows.dtype)], axis=1
            )
        parts.append(part)
    return jnp.concatenate(parts, axis=0)


def swap_matrix(outer, inner):
    total = outer * inner
    row = iota((total, total), 0)
    col = iota((total, total), 1)
    return onehot(col == (row % inner) * outer + row // inner)


def rows_of(messages_ref):
    size = BLOCK * PIECES
    swap = swap_matrix(PIECES, BLOCK)
    blocks = []
    for b in range(messages_ref.shape[0] // size):
        moved = matmul(swap, messages_ref[b * size : (b + 1) * size, :]).astype(BF16)
        blocks.append(
            jnp.concatenate([moved[s * BLOCK : (s + 1) * BLOCK] for s in range(PIECES)], axis=1)
        )
    return jnp.concatenate(blocks, axis=0)


def messages_block(rows, width):
    return matmul(swap_matrix(BLOCK, PIECES), stack_pieces(rows, width))


def spread_kernel(spread_ref):
    count, columns = spread_ref.shape
    spread_ref[...] = onehot(iota((count, columns), 1) % count == iota((count, columns), 0))


def route_kernel(tokens_ref, gain_ref, ids_ref, spread_ref, out_ref, *, experts, width):
    top, count = ids_ref.shape
    columns = PIECES * count
    piece = iota((top, columns), 1) // count
    row = iota((experts * PIECES, columns), 0)
    ids = ids_ref[...].astype(F32).astype(BF16)
    wanted = matmul(ids, spread_ref[...]).astype(jnp.int32) * PIECES + piece
    hit = row == wanted[0:1, :]
    for k in range(1, top):
        hit = jnp.logical_or(hit, row == wanted[k : k + 1, :])
    placing = onehot(hit)
    values = tokens_ref[...].astype(F32)
    scale = lax.rsqrt(jnp.mean(values * values, axis=1, keepdims=True) + epsilon)
    normed = values * scale * gain_ref[...].reshape(1, -1)
    stacked = stack_pieces(normed, width).astype(BF16)
    out_ref[...] = matmul(placing, stacked).astype(BF16)


def tables_kernel(arrived_ref, ids_ref, codes_ref, own_rows, taking, weighing, *, model):
    own_rows[...] = rows_of(arrived_ref)[:, :model]
    ids = ids_ref[...].T
    codes = codes_ref[...].astype(F32)
    weights = (codes / jnp.sum(codes, axis=0, keepdims=True)).T
    count, top = ids.shape
    rows = PIECES * count
    piece = iota((rows, 1), 0) // count
    col = iota((rows, taking.shape[1]), 1)
    for k in range(top):
        here = pl.ds(k * rows, rows)
        wanted = jnp.concatenate([ids[:, k : k + 1]] * PIECES, axis=0) * PIECES + piece
        taking[here, :] = onehot(col == wanted)
        weight = jnp.concatenate([weights[:, k : k + 1]] * PIECES, axis=0)
        weighing[here, :] = jnp.broadcast_to(weight, (rows, weighing.shape[1]))


def expert_kernel(own_rows, other_ref, gate_ref, up_ref, down_ref, own_out, other_out):
    rows, model = own_rows.shape
    x = jnp.concatenate([own_rows[...], rows_of(other_ref)[:, :model]], axis=0)
    gate = lax.dot_general(gate_ref[...], x, NT, preferred_element_type=F32)
    up = lax.dot_general(up_ref[...], x, NT, preferred_element_type=F32)
    hidden = (gate * jax.nn.sigmoid(gate) * up).T.astype(BF16)
    out = matmul(hidden, down_ref[...]).astype(BF16)
    own_out[...] = out[:rows]
    other_out[...] = out[rows:]


def messages_kernel(rows_ref, out_ref, *, width):
    size = BLOCK * PIECES
    for b in range(rows_ref.shape[0] // BLOCK):
        rows = rows_ref[b * BLOCK : (b + 1) * BLOCK, :].astype(F32).astype(BF16)
        out_ref[b * size : (b + 1) * size, :] = messages_block(rows, width).astype(BF16)


def add_kernel(own_ref, arrived_ref, out_ref, *, width):
    size = BLOCK * PIECES
    for b in range(arrived_ref.shape[0] // BLOCK):
        here = pl.ds(b * size, size)
        moved = messages_block(arrived_ref[b * BLOCK : (b + 1) * BLOCK, :], width)
        out_ref[here, :] = (own_ref[here, :].astype(F32) + moved).astype(BF16)


def combine_kernel(tokens_ref, taking, weighing, returned_ref, out_ref, *, width):
    picked = matmul(taking[...], returned_ref[...])
    lanes = weighing.shape[1]
    weight = jnp.concatenate([weighing[...]] * (width // lanes), axis=1)
    weighted = picked * weight
    count, model = tokens_ref.shape
    rows = PIECES * count
    mixture = weighted[:rows]
    for k in range(1, weighted.shape[0] // rows):
        mixture = mixture + weighted[k * rows : (k + 1) * rows]
    for s in range(PIECES):
        span = min((s + 1) * width, model) - s * width
        here = pl.ds(s * width, span)
        out_ref[:, here] = (
            tokens_ref[:, here].astype(F32) + mixture[s * count : (s + 1) * count, :span]
        ).astype(BF16)


VMEM = pl.BlockSpec(memory_space=pltpu.VMEM)
MIB = 1 << 20


def call(kernel, out_shape, args, *, name, mib, flops):
    many = isinstance(out_shape, tuple)
    return pl.pallas_call(
        kernel,
        out_shape=out_shape,
        in_specs=[VMEM] * len(args),
        out_specs=(VMEM,) * len(out_shape) if many else VMEM,
        compiler_params=pltpu.CompilerParams(vmem_limit_bytes=mib * MIB),
        cost_estimate=pl.CostEstimate(flops=flops, bytes_accessed=0, transcendentals=0),
        name=name,
    )(*args)


def shards(tokens, norm_gain, expert_ids, gate_codes, w_gate, w_up, w_down):
    devices = lax.axis_size("ep")
    experts = devices // 2
    count, model = tokens.shape
    top = expert_ids.shape[1]
    width = piece_width(model)
    slots = experts * PIECES
    message = jax.ShapeDtypeStruct((slots, width), BF16)
    rows = jax.ShapeDtypeStruct((experts, model), BF16)
    same_core = [[2 * i + c for i in range(experts)] for c in range(2)]
    partner = [(i, i ^ 1) for i in range(devices)]
    ids = expert_ids.T
    codes = gate_codes.T
    picks = top * PIECES * count

    def exchange(array):
        return lax.all_to_all(
            array.reshape(experts, PIECES, width),
            "ep",
            split_axis=0,
            concat_axis=0,
            axis_index_groups=same_core,
            tiled=True,
        ).reshape(slots, width)

    spread = call(
        spread_kernel,
        jax.ShapeDtypeStruct((count, PIECES * count), BF16),
        (),
        name="spread",
        mib=1,
        flops=5_000_000_000,
    )
    outgoing = call(
        functools.partial(route_kernel, experts=experts, width=width),
        message,
        (tokens, norm_gain, ids, spread),
        name="route",
        mib=4,
        flops=20_000_000_000,
    )
    arrived = exchange(outgoing)
    other = lax.ppermute(arrived, "ep", partner)
    own_rows, taking, weighing = call(
        functools.partial(tables_kernel, model=model),
        (
            rows,
            jax.ShapeDtypeStruct((picks, slots), BF16),
            jax.ShapeDtypeStruct((picks, 128), F32),
        ),
        (arrived, ids, codes),
        name="tables",
        mib=8,
        flops=1_000_000_000,
    )
    own_share, other_share = call(
        expert_kernel,
        (rows, rows),
        (own_rows, other, w_gate[0].T, w_up[0].T, w_down[0]),
        name="expert",
        mib=32,
        flops=2_000_000_000,
    )
    arrived_share = lax.ppermute(other_share, "ep", partner)
    own_messages = call(
        functools.partial(messages_kernel, width=width),
        message,
        (own_share,),
        name="messages",
        mib=8,
        flops=1_000_000_000,
    )
    summed = call(
        functools.partial(add_kernel, width=width),
        message,
        (own_messages, arrived_share),
        name="add",
        mib=8,
        flops=1_000_000,
    )
    return call(
        functools.partial(combine_kernel, width=width),
        jax.ShapeDtypeStruct((count, model), BF16),
        (tokens, taking, weighing, exchange(summed)),
        name="combine",
        mib=8,
        flops=1_000_000,
    )


def solution(mesh):
    return jax.shard_map(
        shards,
        mesh=mesh,
        in_specs=(
            P(("groups", "ep"), None),
            P(),
            P(("groups", "ep"), None),
            P(("groups", "ep"), None),
            P("ep", None, None),
            P("ep", None, None),
            P("ep", None, None),
        ),
        out_specs=P(("groups", "ep"), None),
        check_vma=False,
    )
```

time: 71.9 us -> 69.7 us (0.969)
  local copies, waits for them, and re-layouts: 2.21 us -> 0.78 us
    unnamed x16 -> x20, local copies, waits for them, and re-layouts: 1.5 us -> 0.78 us
    pallas_call x4 -> x7, Pallas kernels: 5.72 us -> 5.58 us  [call(): pl.pallas_call(kernel, out_shape=out_shape, in_specs=[VMEM] * len(args),...]
  transfers between devices with their start and end apart: 2 -> 2, of which waited for: 2 -> 2; matrix products, arithmetic and copies ran while one was open for 0% -> 0% of each run, Pallas kernels for 0% -> 1%
where the time goes in v2:
time: 69.7 us; the launch traced here: 69.6 us
  blocking collectives  60.1 us (86%)
  Pallas kernels  5.58 us (8%)
  waiting for transfers between devices  2.69 us (4%)
  local copies, waits for them, and re-layouts  0.78 us (1%)
    all_to_all x2, blocking collectives, exchange(): lax.all_to_all(array.reshape(experts, PIECES, width), 'ep', split_axis=0,...  60.1 us
    pallas_call x7, Pallas kernels, call(): pl.pallas_call(kernel, out_shape=out_shape, in_specs=[VMEM] * len(args),...  5.58 us
    ppermute x1, waiting for transfers between devices, shards(): other = lax.ppermute(arrived, 'ep', partner)  1.42 us
  transfers between devices with their start and end apart: 2, of which 2 were waited for; matrix products, arithmetic and copies ran while one was open for 0% of the time, Pallas kernels for 1%

profile of v2, /device:TPU:514, one launch (start us, length us, event | category | flops | bytes accessed | tf_op | source)
XLA Modules:
  0.0 69.6 jit_solution(7894931090787142079)
XLA Ops:
  0.0 0.0 copy-start
  0.0 0.0 copy-start.2
  0.0 0.0 copy-start.1
  0.0 0.0 slice-start
  0.0 0.0 slice-start.2
  0.0 0.0 slice-start.4
  0.1 0.7 %copy-done = bf16[8,2880]{1,0:T(8,128)(2,1)S(1)} copy-done((bf16[8,2880]{1,0:T(8,128)(2,1)S(1)}, bf16[8,2880]{1,0:T(8,128)(2,1)}, u32[]{:S(2)}) %copy-start) | copy-done | bytes 46104
  0.8 0.0 copy-done.2
  0.8 0.0 copy-done.1
  0.8 0.0 copy-start.3
  0.8 0.0 slice-start.1
  0.8 0.0 slice-start.3
  0.8 0.0 slice-start.5
  0.8 0.4 route.1
  1.2 37.9 %all_to_all.10 = bf16[64,8,384]{2,1,0:T(8,128)(2,1)S(1)} all-to-all(bf16[64,8,384]{2,1,0:T(8,128)(2,1)S(1)} %bitcast.26), channel_id=1, replica_groups={{0,2,4,6,8,10,12,14,16,18,20,22,24,26,28,30,32,34,36,38,40,42,44,46,48,..., dimensions={0} | all-to-all | bytes 786432 | tf_op jit(solution)/shard_map/all_to_all | solution.py:187
  39.1 0.0 collective-permute-start
  39.1 0.0 copy-done.3
  39.1 0.3 tables.1
  39.4 1.4 %collective-permute-done.other_ref = bf16[512,384]{1,0:T(8,128)(2,1)S(1)} collective-permute-done((bf16[512,384]{1,0:T(8,128)(2,1)S(1)}, bf16[512,384]{1,0:T(8,128)(2,1)S(1)}, u32[]{:S(2)}, u32[]{:S(2)}) %collective-permute-start) | collective-permute-done | bytes 393248 | tf_op jit(solution)/shard_map/ppermute | solution.py:213
  40.8 0.0 slice-done
  40.8 0.0 slice-done.2
  40.8 0.0 slice-done.4
  40.8 0.0 slice-done.1
  40.8 0.0 slice-done.3
  40.8 0.0 slice-done.5
  40.9 3.4 %expert.1 = (bf16[64,2880]{1,0:T(8,128)(2,1)S(1)}, bf16[64,2880]{1,0:T(8,128)(2,1)S(1)}) custom-call(bf16[64,2880]{1,0:T(8,128)(2,1)S(1)} %get-tuple-element.12.own_rows, bf16[512,384]{1,0:T(8,128)(2,1)S(1)} %collective-permute-done.other_ref, bf16[720,2880]{1,0:T(8,128)(2,1)S(1)} %bitcast.15, bf16[720,2880]{1,0:T(8,128)(2,1)S(1)} %bitcast.18, ...), custom_call_target="tpu_custom_call" | custom-call | flops 2000000000 | tf_op jit(solution)/shard_map/expert/pallas_call | solution.py:160
  44.3 0.3 collective-permute-start.1
  44.5 0.3 messages.1.own_ref
  44.8 1.3 %collective-permute-done.1.arrived_ref = bf16[64,2880]{1,0:T(8,128)(2,1)S(1)} collective-permute-done((bf16[64,2880]{1,0:T(8,128)(2,1)S(1)}, bf16[64,2880]{1,0:T(8,128)(2,1)S(1)}, u32[]{:S(2)}, u32[]{:S(2)}) %collective-permute-start.1) | collective-permute-done | bytes 368672 | tf_op jit(solution)/shard_map/ppermute | solution.py:234
  46.1 0.3 add.1
  46.4 22.2 %all_to_all.11 = bf16[64,8,384]{2,1,0:T(8,128)(2,1)S(1)} all-to-all(bf16[64,8,384]{2,1,0:T(8,128)(2,1)S(1)} %bitcast.23), channel_id=1, replica_groups={{0,2,4,6,8,10,12,14,16,18,20,22,24,26,28,30,32,34,36,38,40,42,44,46,48,..., dimensions={0} | all-to-all | bytes 786432 | tf_op jit(solution)/shard_map/all_to_all | solution.py:187
  68.6 0.9 %combine.1 = bf16[8,2880]{1,0:T(8,128)(2,1)} custom-call(bf16[8,2880]{1,0:T(8,128)(2,1)S(1)} %copy-done, bf16[256,512]{1,0:T(8,128)(2,1)S(1)} %get-tuple-element.10.taking, f32[256,128]{1,0:T(8,128)S(1)} %get-tuple-element.11.weighing, bf16[512,384]{1,0:T(8,128)(2,1)S(1)} %bitcast.22), custom_call_target="tpu_custom_call" | custom-call | flops 1000000 | tf_op jit(solution)/shard_map/combine/pallas_call | solution.py:160
  (4 shorter events, 0.0 us)
Async XLA Ops:
  0.0 0.8 %copy-start = (bf16[8,2880]{1,0:T(8,128)(2,1)S(1)}, bf16[8,2880]{1,0:T(8,128)(2,1)}, u32[]{:S(2)}) copy-start(bf16[8,2880]{1,0:T(8,128)(2,1)} %tokens_ref.3) | copy-start | bytes 138244
  0.0 0.8 %copy-start.2 = (s32[8,4]{0,1:T(4,128)S(1)}, s32[8,4]{0,1:T(4,128)}, u32[]{:S(2)}) copy-start(s32[8,4]{0,1:T(4,128)} %param.9) | copy-start | bytes 388
  0.0 0.8 %copy-start.1 = (f32[2880]{0:T(1024)S(1)}, f32[2880]{0:T(1024)}, u32[]{:S(2)}) copy-start(f32[2880]{0:T(1024)} %gain_ref.1) | copy-start | bytes 34564
  0.0 40.8 %slice-start = ((s8[4239360]{0:T(1024)(128)(4,1)}), s8[4194304]{0:T(1024)(128)(4,1)S(1)}, s32[]{:S(2)}) async-start(s8[4239360]{0:T(1024)(128)(4,1)} %bitcast.13), calls=%async_computation.2 | async-start | bytes 8388608
  0.0 40.8 %slice-start.2 = ((s8[4239360]{0:T(1024)(128)(4,1)}), s8[4194304]{0:T(1024)(128)(4,1)S(1)}, s32[]{:S(2)}) async-start(s8[4239360]{0:T(1024)(128)(4,1)} %bitcast.16), calls=%async_computation.4 | async-start | bytes 8388608
  0.0 40.8 %slice-start.4 = ((s8[4239360]{0:T(1024)(128)(4,1)}), s8[4194304]{0:T(1024)(128)(4,1)S(1)}, s32[]{:S(2)}) async-start(s8[4239360]{0:T(1024)(128)(4,1)} %bitcast.19), calls=%async_computation.6 | async-start | bytes 8388608
  0.8 38.3 %copy-start.3 = (s32[8,4]{0,1:T(4,128)S(1)}, s32[8,4]{0,1:T(4,128)}, u32[]{:S(2)}) copy-start(s32[8,4]{0,1:T(4,128)} %param.10) | copy-start | bytes 388
  0.8 40.0 %slice-start.1 = ((s8[4239360]{0:T(1024)(128)(4,1)}), s8[45056]{0:T(1024)(128)(4,1)S(1)}, s32[]{:S(2)}) async-start(s8[4239360]{0:T(1024)(128)(4,1)} %bitcast.13), calls=%async_computation.3 | async-start | bytes 90112
  0.8 40.0 %slice-start.3 = ((s8[4239360]{0:T(1024)(128)(4,1)}), s8[45056]{0:T(1024)(128)(4,1)S(1)}, s32[]{:S(2)}) async-start(s8[4239360]{0:T(1024)(128)(4,1)} %bitcast.16), calls=%async_computation.5 | async-start | bytes 90112
  0.8 40.0 %slice-start.5 = ((s8[4239360]{0:T(1024)(128)(4,1)}), s8[45056]{0:T(1024)(128)(4,1)S(1)}, s32[]{:S(2)}) async-start(s8[4239360]{0:T(1024)(128)(4,1)} %bitcast.19), calls=%async_computation.7 | async-start | bytes 90112
  39.1 1.7 %collective-permute-start = (bf16[512,384]{1,0:T(8,128)(2,1)S(1)}, bf16[512,384]{1,0:T(8,128)(2,1)S(1)}, u32[]{:S(2)}, u32[]{:S(2)}) collective-permute-start(bf16[512,384]{1,0:T(8,128)(2,1)S(1)} %bitcast.24), channel_id=1, source_target_pairs={{0,1},{1,0},{2,3},{3,2},{4,5},{5,4},{6,7},{7,6},{8,9},{9,8},{10,11... | collective-permute-start | bytes 1179656 | tf_op jit(solution)/shard_map/ppermute | solution.py:213
  44.3 1.8 %collective-permute-start.1 = (bf16[64,2880]{1,0:T(8,128)(2,1)S(1)}, bf16[64,2880]{1,0:T(8,128)(2,1)S(1)}, u32[]{:S(2)}, u32[]{:S(2)}) collective-permute-start(bf16[64,2880]{1,0:T(8,128)(2,1)S(1)} %get-tuple-element.14), channel_id=1, source_target_pairs={{0,1},{1,0},{2,3},{3,2},{4,5},{5,4},{6,7},{7,6},{8,9},{9,8},{10,11... | collective-permute-start | bytes 1105928 | tf_op jit(solution)/shard_map/ppermute | solution.py:234

commit v3 on v2

--- a/solution.py
+++ b/solution.py
@@ -107,21 +107,21 @@
         weighing[here, :] = jnp.broadcast_to(weight, (rows, weighing.shape[1]))
 
 
-def expert_kernel(own_rows, other_ref, gate_ref, up_ref, down_ref, own_out, other_out):
+def expert_kernel(own_rows, other_ref, gate_ref, up_ref, down_ref, own_hidden, other_out):
     rows, model = own_rows.shape
-    x = jnp.concatenate([own_rows[...], rows_of(other_ref)[:, :model]], axis=0)
+    x = jnp.concatenate([rows_of(other_ref)[:, :model], own_rows[...]], axis=0)
     gate = lax.dot_general(gate_ref[...], x, NT, preferred_element_type=F32)
     up = lax.dot_general(up_ref[...], x, NT, preferred_element_type=F32)
     hidden = (gate * jax.nn.sigmoid(gate) * up).T.astype(BF16)
-    out = matmul(hidden, down_ref[...]).astype(BF16)
-    own_out[...] = out[:rows]
-    other_out[...] = out[rows:]
-
-
-def messages_kernel(rows_ref, out_ref, *, width):
+    own_hidden[...] = hidden[rows:]
+    other_out[...] = matmul(hidden[:rows], down_ref[...]).astype(BF16)
+
+
+def own_kernel(hidden_ref, down_ref, out_ref, *, width):
     size = BLOCK * PIECES
-    for b in range(rows_ref.shape[0] // BLOCK):
-        rows = rows_ref[b * BLOCK : (b + 1) * BLOCK, :].astype(F32).astype(BF16)
+    share = matmul(hidden_ref[...], down_ref[...]).astype(BF16)
+    for b in range(share.shape[0] // BLOCK):
+        rows = share[b * BLOCK : (b + 1) * BLOCK]
         out_ref[b * size : (b + 1) * size, :] = messages_block(rows, width).astype(BF16)
 
 
@@ -223,9 +223,9 @@
         mib=8,
         flops=1_000_000_000,
     )
-    own_share, other_share = call(
+    own_hidden, other_share = call(
         expert_kernel,
-        (rows, rows),
+        (jax.ShapeDtypeStruct((experts, w_down.shape[1]), BF16), rows),
         (own_rows, other, w_gate[0].T, w_up[0].T, w_down[0]),
         name="expert",
         mib=32,
@@ -233,11 +233,11 @@
     )
     arrived_share = lax.ppermute(other_share, "ep", partner)
     own_messages = call(
-        functools.partial(messages_kernel, width=width),
+        functools.partial(own_kernel, width=width),
         message,
-        (own_share,),
-        name="messages",
-        mib=8,
+        (own_hidden, w_down[0]),
+        name="own",
+        mib=16,
         flops=1_000_000_000,
     )
     summed = call(

time: 69.7 us -> 69.8 us (level)
  Pallas kernels: 5.58 us -> 6.55 us
  waiting for transfers between devices: 2.69 us -> 1.84 us
    pallas_call x7, Pallas kernels: 5.58 us -> 6.55 us  [call(): pl.pallas_call(kernel, out_shape=out_shape, in_specs=[VMEM] * len(args),...]
    ppermute x1, waiting for transfers between devices: 1.27 us -> 0.42 us  [shards(): arrived_share = lax.ppermute(other_share, 'ep', partner)]
  transfers between devices with their start and end apart: 2 -> 2, of which waited for: 2 -> 2; matrix products, arithmetic and copies ran while one was open for 0% -> 0% of each run, Pallas kernels for 1% -> 2%
where the time goes in v3:
time: 69.8 us; the launch traced here: 69.7 us
  blocking collectives  60.1 us (86%)
  Pallas kernels  6.55 us (9%)
  waiting for transfers between devices  1.84 us (3%)
  local copies, waits for them, and re-layouts  0.78 us (1%)
    all_to_all x2, blocking collectives, exchange(): lax.all_to_all(array.reshape(experts, PIECES, width), 'ep', split_axis=0,...  60.1 us
    pallas_call x7, Pallas kernels, call(): pl.pallas_call(kernel, out_shape=out_shape, in_specs=[VMEM] * len(args),...  6.55 us
    ppermute x1, waiting for transfers between devices, shards(): other = lax.ppermute(arrived, 'ep', partner)  1.42 us
  transfers between devices with their start and end apart: 2, of which 2 were waited for; matrix products, arithmetic and copies ran while one was open for 0% of the time, Pallas kernels for 2%

profile of v3, /device:TPU:514, one launch (start us, length us, event | category | flops | bytes accessed | tf_op | source)
XLA Modules:
  0.0 69.7 jit_solution(7583455777913547240)
XLA Ops:
  0.0 0.0 copy-start
  0.0 0.0 copy-start.2
  0.0 0.0 copy-start.1
  0.0 0.0 slice-start
  0.0 0.0 slice-start.2
  0.0 0.0 slice-start.4
  0.1 0.7 %copy-done = bf16[8,2880]{1,0:T(8,128)(2,1)S(1)} copy-done((bf16[8,2880]{1,0:T(8,128)(2,1)S(1)}, bf16[8,2880]{1,0:T(8,128)(2,1)}, u32[]{:S(2)}) %copy-start) | copy-done | bytes 46104
  0.8 0.0 copy-done.2
  0.8 0.0 copy-done.1
  0.8 0.0 copy-start.3
  0.8 0.0 slice-start.1
  0.8 0.0 slice-start.3
  0.8 0.0 slice-start.5
  0.8 0.4 route.1
  1.2 37.9 %all_to_all.10 = bf16[64,8,384]{2,1,0:T(8,128)(2,1)S(1)} all-to-all(bf16[64,8,384]{2,1,0:T(8,128)(2,1)S(1)} %bitcast.27), channel_id=1, replica_groups={{0,2,4,6,8,10,12,14,16,18,20,22,24,26,28,30,32,34,36,38,40,42,44,46,48,..., dimensions={0} | all-to-all | bytes 786432 | tf_op jit(solution)/shard_map/all_to_all | solution.py:187
  39.1 0.0 collective-permute-start
  39.1 0.0 copy-done.3
  39.1 0.3 tables.1
  39.4 1.4 %collective-permute-done.other_ref = bf16[512,384]{1,0:T(8,128)(2,1)S(1)} collective-permute-done((bf16[512,384]{1,0:T(8,128)(2,1)S(1)}, bf16[512,384]{1,0:T(8,128)(2,1)S(1)}, u32[]{:S(2)}, u32[]{:S(2)}) %collective-permute-start) | collective-permute-done | bytes 393248 | tf_op jit(solution)/shard_map/ppermute | solution.py:213
  40.8 0.0 slice-done
  40.8 0.0 slice-done.2
  40.8 0.0 slice-done.4
  40.8 0.0 slice-done.1
  40.8 0.0 slice-done.3
  40.8 0.0 slice-done.5
  40.9 3.5 %expert.1 = (bf16[64,720]{1,0:T(8,128)(2,1)S(1)}, bf16[64,2880]{1,0:T(8,128)(2,1)S(1)}) custom-call(bf16[64,2880]{1,0:T(8,128)(2,1)S(1)} %get-tuple-element.12.own_rows, bf16[512,384]{1,0:T(8,128)(2,1)S(1)} %collective-permute-done.other_ref, bf16[720,2880]{1,0:T(8,128)(2,1)S(1)} %bitcast.19, bf16[720,2880]{1,0:T(8,128)(2,1)S(1)} %bitcast.22, ...), custom_call_target="tpu_custom_call" | custom-call | flops 2000000000 | tf_op jit(solution)/shard_map/expert/pallas_call | solution.py:160
  44.4 0.2 collective-permute-start.1
  44.6 1.2 %own.1.own_ref = bf16[512,384]{1,0:T(8,128)(2,1)S(1)} custom-call(bf16[64,720]{1,0:T(8,128)(2,1)S(1)} %get-tuple-element.13.hidden_ref, bf16[720,2880]{1,0:T(8,128)(2,1)S(1)} %bitcast.16), custom_call_target="tpu_custom_call" | custom-call | flops 1000000000 | tf_op jit(solution)/shard_map/own/pallas_call | solution.py:160
  45.8 0.4 collective-permute-done.1.arrived_ref
  46.2 0.3 add.1
  46.5 22.2 %all_to_all.11 = bf16[64,8,384]{2,1,0:T(8,128)(2,1)S(1)} all-to-all(bf16[64,8,384]{2,1,0:T(8,128)(2,1)S(1)} %bitcast.24), channel_id=1, replica_groups={{0,2,4,6,8,10,12,14,16,18,20,22,24,26,28,30,32,34,36,38,40,42,44,46,48,..., dimensions={0} | all-to-all | bytes 786432 | tf_op jit(solution)/shard_map/all_to_all | solution.py:187
  68.7 0.9 %combine.1 = bf16[8,2880]{1,0:T(8,128)(2,1)} custom-call(bf16[8,2880]{1,0:T(8,128)(2,1)S(1)} %copy-done, bf16[256,512]{1,0:T(8,128)(2,1)S(1)} %get-tuple-element.10.taking, f32[256,128]{1,0:T(8,128)S(1)} %get-tuple-element.11.weighing, bf16[512,384]{1,0:T(8,128)(2,1)S(1)} %bitcast.23), custom_call_target="tpu_custom_call" | custom-call | flops 1000000 | tf_op jit(solution)/shard_map/combine/pallas_call | solution.py:160
  (4 shorter events, 0.0 us)
Async XLA Ops:
  0.0 0.8 %copy-start = (bf16[8,2880]{1,0:T(8,128)(2,1)S(1)}, bf16[8,2880]{1,0:T(8,128)(2,1)}, u32[]{:S(2)}) copy-start(bf16[8,2880]{1,0:T(8,128)(2,1)} %tokens_ref.3) | copy-start | bytes 138244
  0.0 0.8 %copy-start.2 = (s32[8,4]{0,1:T(4,128)S(1)}, s32[8,4]{0,1:T(4,128)}, u32[]{:S(2)}) copy-start(s32[8,4]{0,1:T(4,128)} %param.9) | copy-start | bytes 388
  0.0 0.8 %copy-start.1 = (f32[2880]{0:T(1024)S(1)}, f32[2880]{0:T(1024)}, u32[]{:S(2)}) copy-start(f32[2880]{0:T(1024)} %gain_ref.1) | copy-start | bytes 34564
  0.0 40.8 %slice-start = ((s8[4239360]{0:T(1024)(128)(4,1)}), s8[4194304]{0:T(1024)(128)(4,1)S(1)}, s32[]{:S(2)}) async-start(s8[4239360]{0:T(1024)(128)(4,1)} %bitcast.13), calls=%async_computation.2 | async-start | bytes 8388608
  0.0 40.8 %slice-start.2 = ((s8[4239360]{0:T(1024)(128)(4,1)}), s8[4194304]{0:T(1024)(128)(4,1)S(1)}, s32[]{:S(2)}) async-start(s8[4239360]{0:T(1024)(128)(4,1)} %bitcast.17), calls=%async_computation.4 | async-start | bytes 8388608
  0.0 40.8 %slice-start.4 = ((s8[4239360]{0:T(1024)(128)(4,1)}), s8[4194304]{0:T(1024)(128)(4,1)S(1)}, s32[]{:S(2)}) async-start(s8[4239360]{0:T(1024)(128)(4,1)} %bitcast.20), calls=%async_computation.6 | async-start | bytes 8388608
  0.8 38.3 %copy-start.3 = (s32[8,4]{0,1:T(4,128)S(1)}, s32[8,4]{0,1:T(4,128)}, u32[]{:S(2)}) copy-start(s32[8,4]{0,1:T(4,128)} %param.10) | copy-start | bytes 388
  0.8 40.0 %slice-start.1 = ((s8[4239360]{0:T(1024)(128)(4,1)}), s8[45056]{0:T(1024)(128)(4,1)S(1)}, s32[]{:S(2)}) async-start(s8[4239360]{0:T(1024)(128)(4,1)} %bitcast.13), calls=%async_computation.3 | async-start | bytes 90112
  0.8 40.0 %slice-start.3 = ((s8[4239360]{0:T(1024)(128)(4,1)}), s8[45056]{0:T(1024)(128)(4,1)S(1)}, s32[]{:S(2)}) async-start(s8[4239360]{0:T(1024)(128)(4,1)} %bitcast.17), calls=%async_computation.5 | async-start | bytes 90112
  0.8 40.0 %slice-start.5 = ((s8[4239360]{0:T(1024)(128)(4,1)}), s8[45056]{0:T(1024)(128)(4,1)S(1)}, s32[]{:S(2)}) async-start(s8[4239360]{0:T(1024)(128)(4,1)} %bitcast.20), calls=%async_computation.7 | async-start | bytes 90112
  39.1 1.7 %collective-permute-start = (bf16[512,384]{1,0:T(8,128)(2,1)S(1)}, bf16[512,384]{1,0:T(8,128)(2,1)S(1)}, u32[]{:S(2)}, u32[]{:S(2)}) collective-permute-start(bf16[512,384]{1,0:T(8,128)(2,1)S(1)} %bitcast.25), channel_id=1, source_target_pairs={{0,1},{1,0},{2,3},{3,2},{4,5},{5,4},{6,7},{7,6},{8,9},{9,8},{10,11... | collective-permute-start | bytes 1179656 | tf_op jit(solution)/shard_map/ppermute | solution.py:213
  44.4 1.8 %collective-permute-start.1 = (bf16[64,2880]{1,0:T(8,128)(2,1)S(1)}, bf16[64,2880]{1,0:T(8,128)(2,1)S(1)}, u32[]{:S(2)}, u32[]{:S(2)}) collective-permute-start(bf16[64,2880]{1,0:T(8,128)(2,1)S(1)} %get-tuple-element.14), channel_id=1, source_target_pairs={{0,1},{1,0},{2,3},{3,2},{4,5},{5,4},{6,7},{7,6},{8,9},{9,8},{10,11... | collective-permute-start | bytes 1105928 | tf_op jit(solution)/shard_map/ppermute | solution.py:234

commit v4 on v2

--- a/solution.py
+++ b/solution.py
@@ -1,4 +1,5 @@
 import functools
+import math
 
 import jax
 import jax.numpy as jnp
@@ -25,6 +26,13 @@
 
 def matmul(a, b):
     return jnp.dot(a, b, preferred_element_type=F32)
+
+
+def place(expert, experts):
+    side = math.isqrt(experts)
+    half = side // 2
+    row, column = expert // side, expert % side
+    return (row + half * (column // half)) % side * side + column
 
 
 def piece_width(model_width):
@@ -78,7 +86,7 @@
     piece = iota((top, columns), 1) // count
     row = iota((experts * PIECES, columns), 0)
     ids = ids_ref[...].astype(F32).astype(BF16)
-    wanted = matmul(ids, spread_ref[...]).astype(jnp.int32) * PIECES + piece
+    wanted = place(matmul(ids, spread_ref[...]).astype(jnp.int32), experts) * PIECES + piece
     hit = row == wanted[0:1, :]
     for k in range(1, top):
         hit = jnp.logical_or(hit, row == wanted[k : k + 1, :])
@@ -92,7 +100,7 @@
 
 def tables_kernel(arrived_ref, ids_ref, codes_ref, own_rows, taking, weighing, *, model):
     own_rows[...] = rows_of(arrived_ref)[:, :model]
-    ids = ids_ref[...].T
+    ids = place(ids_ref[...], taking.shape[1] // PIECES).T
     codes = codes_ref[...].astype(F32)
     weights = (codes / jnp.sum(codes, axis=0, keepdims=True)).T
     count, top = ids.shape
@@ -177,7 +185,7 @@
     slots = experts * PIECES
     message = jax.ShapeDtypeStruct((slots, width), BF16)
     rows = jax.ShapeDtypeStruct((experts, model), BF16)
-    same_core = [[2 * i + c for i in range(experts)] for c in range(2)]
+    same_core = [[2 * place(i, experts) + c for i in range(experts)] for c in range(2)]
     partner = [(i, i ^ 1) for i in range(devices)]
     ids = expert_ids.T
     codes = gate_codes.T

time: 69.7 us -> 68.8 us (0.987)
  blocking collectives: 60.1 us -> 59.2 us
    all_to_all x2, blocking collectives: 60.1 us -> 59.2 us  [exchange(): lax.all_to_all(array.reshape(experts, PIECES, width), 'ep', split_axis=0,...]
where the time goes in v4:
time: 68.8 us; the launch traced here: 68.6 us
  blocking collectives  59.2 us (86%)
  Pallas kernels  5.6 us (8%)
  waiting for transfers between devices  2.69 us (4%)
  local copies, waits for them, and re-layouts  0.78 us (1%)
    all_to_all x2, blocking collectives, exchange(): lax.all_to_all(array.reshape(experts, PIECES, width), 'ep', split_axis=0,...  59.2 us
    pallas_call x7, Pallas kernels, call(): pl.pallas_call(kernel, out_shape=out_shape, in_specs=[VMEM] * len(args),...  5.6 us
    ppermute x1, waiting for transfers between devices, shards(): other = lax.ppermute(arrived, 'ep', partner)  1.43 us
  transfers between devices with their start and end apart: 2, of which 2 were waited for; matrix products, arithmetic and copies ran while one was open for 0% of the time, Pallas kernels for 1%

profile of v4, /device:TPU:514, one launch (start us, length us, event | category | flops | bytes accessed | tf_op | source)
XLA Modules:
  0.0 68.6 jit_solution(9144244610215739016)
XLA Ops:
  0.0 0.0 copy-start
  0.0 0.0 copy-start.2
  0.0 0.0 copy-start.1
  0.0 0.0 slice-start
  0.0 0.0 slice-start.2
  0.0 0.0 slice-start.4
  0.1 0.7 %copy-done = bf16[8,2880]{1,0:T(8,128)(2,1)S(1)} copy-done((bf16[8,2880]{1,0:T(8,128)(2,1)S(1)}, bf16[8,2880]{1,0:T(8,128)(2,1)}, u32[]{:S(2)}) %copy-start) | copy-done | bytes 46104
  0.8 0.0 copy-done.2
  0.8 0.0 copy-done.1
  0.8 0.0 copy-start.3
  0.8 0.0 slice-start.1
  0.8 0.0 slice-start.3
  0.8 0.0 slice-start.5
  0.8 0.4 route.1
  1.2 36.6 %all_to_all.10 = bf16[64,8,384]{2,1,0:T(8,128)(2,1)S(1)} all-to-all(bf16[64,8,384]{2,1,0:T(8,128)(2,1)S(1)} %bitcast.26), channel_id=1, replica_groups={{0,2,4,6,72,74,76,78,16,18,20,22,88,90,92,94,32,34,36,38,104,106,108,11..., dimensions={0} | all-to-all | bytes 786432 | tf_op jit(solution)/shard_map/all_to_all | solution.py:195
  37.8 0.0 collective-permute-start
  37.8 0.0 copy-done.3
  37.8 0.3 tables.1
  38.1 1.4 %collective-permute-done.other_ref = bf16[512,384]{1,0:T(8,128)(2,1)S(1)} collective-permute-done((bf16[512,384]{1,0:T(8,128)(2,1)S(1)}, bf16[512,384]{1,0:T(8,128)(2,1)S(1)}, u32[]{:S(2)}, u32[]{:S(2)}) %collective-permute-start) | collective-permute-done | bytes 393248 | tf_op jit(solution)/shard_map/ppermute | solution.py:221
  39.5 0.0 slice-done
  39.5 0.0 slice-done.2
  39.5 0.0 slice-done.4
  39.5 0.0 slice-done.1
  39.5 0.0 slice-done.3
  39.5 0.0 slice-done.5
  39.6 3.4 %expert.1 = (bf16[64,2880]{1,0:T(8,128)(2,1)S(1)}, bf16[64,2880]{1,0:T(8,128)(2,1)S(1)}) custom-call(bf16[64,2880]{1,0:T(8,128)(2,1)S(1)} %get-tuple-element.12.own_rows, bf16[512,384]{1,0:T(8,128)(2,1)S(1)} %collective-permute-done.other_ref, bf16[720,2880]{1,0:T(8,128)(2,1)S(1)} %bitcast.15, bf16[720,2880]{1,0:T(8,128)(2,1)S(1)} %bitcast.18, ...), custom_call_target="tpu_custom_call" | custom-call | flops 2000000000 | tf_op jit(solution)/shard_map/expert/pallas_call | solution.py:168
  43.0 0.3 collective-permute-start.1
  43.2 0.3 messages.1.own_ref
  43.5 1.3 %collective-permute-done.1.arrived_ref = bf16[64,2880]{1,0:T(8,128)(2,1)S(1)} collective-permute-done((bf16[64,2880]{1,0:T(8,128)(2,1)S(1)}, bf16[64,2880]{1,0:T(8,128)(2,1)S(1)}, u32[]{:S(2)}, u32[]{:S(2)}) %collective-permute-start.1) | collective-permute-done | bytes 368672 | tf_op jit(solution)/shard_map/ppermute | solution.py:242
  44.8 0.3 add.1
  45.1 22.6 %all_to_all.11 = bf16[64,8,384]{2,1,0:T(8,128)(2,1)S(1)} all-to-all(bf16[64,8,384]{2,1,0:T(8,128)(2,1)S(1)} %bitcast.23), channel_id=1, replica_groups={{0,2,4,6,72,74,76,78,16,18,20,22,88,90,92,94,32,34,36,38,104,106,108,11..., dimensions={0} | all-to-all | bytes 786432 | tf_op jit(solution)/shard_map/all_to_all | solution.py:195
  67.7 0.9 %combine.1 = bf16[8,2880]{1,0:T(8,128)(2,1)} custom-call(bf16[8,2880]{1,0:T(8,128)(2,1)S(1)} %copy-done, bf16[256,512]{1,0:T(8,128)(2,1)S(1)} %get-tuple-element.10.taking, f32[256,128]{1,0:T(8,128)S(1)} %get-tuple-element.11.weighing, bf16[512,384]{1,0:T(8,128)(2,1)S(1)} %bitcast.22), custom_call_target="tpu_custom_call" | custom-call | flops 1000000 | tf_op jit(solution)/shard_map/combine/pallas_call | solution.py:168
  (4 shorter events, 0.0 us)
Async XLA Ops:
  0.0 0.8 %copy-start = (bf16[8,2880]{1,0:T(8,128)(2,1)S(1)}, bf16[8,2880]{1,0:T(8,128)(2,1)}, u32[]{:S(2)}) copy-start(bf16[8,2880]{1,0:T(8,128)(2,1)} %tokens_ref.3) | copy-start | bytes 138244
  0.0 0.8 %copy-start.2 = (s32[8,4]{0,1:T(4,128)S(1)}, s32[8,4]{0,1:T(4,128)}, u32[]{:S(2)}) copy-start(s32[8,4]{0,1:T(4,128)} %param.9) | copy-start | bytes 388
  0.0 0.8 %copy-start.1 = (f32[2880]{0:T(1024)S(1)}, f32[2880]{0:T(1024)}, u32[]{:S(2)}) copy-start(f32[2880]{0:T(1024)} %gain_ref.1) | copy-start | bytes 34564
  0.0 39.5 %slice-start = ((s8[4239360]{0:T(1024)(128)(4,1)}), s8[4194304]{0:T(1024)(128)(4,1)S(1)}, s32[]{:S(2)}) async-start(s8[4239360]{0:T(1024)(128)(4,1)} %bitcast.13), calls=%async_computation.2 | async-start | bytes 8388608
  0.0 39.5 %slice-start.2 = ((s8[4239360]{0:T(1024)(128)(4,1)}), s8[4194304]{0:T(1024)(128)(4,1)S(1)}, s32[]{:S(2)}) async-start(s8[4239360]{0:T(1024)(128)(4,1)} %bitcast.16), calls=%async_computation.4 | async-start | bytes 8388608
  0.0 39.5 %slice-start.4 = ((s8[4239360]{0:T(1024)(128)(4,1)}), s8[4194304]{0:T(1024)(128)(4,1)S(1)}, s32[]{:S(2)}) async-start(s8[4239360]{0:T(1024)(128)(4,1)} %bitcast.19), calls=%async_computation.6 | async-start | bytes 8388608
  0.8 37.0 %copy-start.3 = (s32[8,4]{0,1:T(4,128)S(1)}, s32[8,4]{0,1:T(4,128)}, u32[]{:S(2)}) copy-start(s32[8,4]{0,1:T(4,128)} %param.10) | copy-start | bytes 388
  0.8 38.7 %slice-start.1 = ((s8[4239360]{0:T(1024)(128)(4,1)}), s8[45056]{0:T(1024)(128)(4,1)S(1)}, s32[]{:S(2)}) async-start(s8[4239360]{0:T(1024)(128)(4,1)} %bitcast.13), calls=%async_computation.3 | async-start | bytes 90112
  0.8 38.7 %slice-start.3 = ((s8[4239360]{0:T(1024)(128)(4,1)}), s8[45056]{0:T(1024)(128)(4,1)S(1)}, s32[]{:S(2)}) async-start(s8[4239360]{0:T(1024)(128)(4,1)} %bitcast.16), calls=%async_computation.5 | async-start | bytes 90112
  0.8 38.7 %slice-start.5 = ((s8[4239360]{0:T(1024)(128)(4,1)}), s8[45056]{0:T(1024)(128)(4,1)S(1)}, s32[]{:S(2)}) async-start(s8[4239360]{0:T(1024)(128)(4,1)} %bitcast.19), calls=%async_computation.7 | async-start | bytes 90112
  37.8 1.7 %collective-permute-start = (bf16[512,384]{1,0:T(8,128)(2,1)S(1)}, bf16[512,384]{1,0:T(8,128)(2,1)S(1)}, u32[]{:S(2)}, u32[]{:S(2)}) collective-permute-start(bf16[512,384]{1,0:T(8,128)(2,1)S(1)} %bitcast.24), channel_id=1, source_target_pairs={{0,1},{1,0},{2,3},{3,2},{4,5},{5,4},{6,7},{7,6},{8,9},{9,8},{10,11... | collective-permute-start | bytes 1179656 | tf_op jit(solution)/shard_map/ppermute | solution.py:221
  43.0 1.8 %collective-permute-start.1 = (bf16[64,2880]{1,0:T(8,128)(2,1)S(1)}, bf16[64,2880]{1,0:T(8,128)(2,1)S(1)}, u32[]{:S(2)}, u32[]{:S(2)}) collective-permute-start(bf16[64,2880]{1,0:T(8,128)(2,1)S(1)} %get-tuple-element.14), channel_id=1, source_target_pairs={{0,1},{1,0},{2,3},{3,2},{4,5},{5,4},{6,7},{7,6},{8,9},{9,8},{10,11... | collective-permute-start | bytes 1105928 | tf_op jit(solution)/shard_map/ppermute | solution.py:242

commit v5 on v4

--- a/solution.py
+++ b/solution.py
@@ -10,7 +10,7 @@
 
 epsilon = 1e-05
 PIECES = 8
-BLOCK = 32
+BLOCK = 16
 NT = (((1,), (1,)), ((), ()))
 F32 = jnp.float32
 BF16 = jnp.bfloat16
@@ -129,7 +129,7 @@
 def messages_kernel(rows_ref, out_ref, *, width):
     size = BLOCK * PIECES
     for b in range(rows_ref.shape[0] // BLOCK):
-        rows = rows_ref[b * BLOCK : (b + 1) * BLOCK, :].astype(F32).astype(BF16)
+        rows = rows_ref[b * BLOCK : (b + 1) * BLOCK, :]
         out_ref[b * size : (b + 1) * size, :] = messages_block(rows, width).astype(BF16)
 
 

time: 68.8 us -> 68.7 us (level)
  no operation moved by 1% of the time
where the time goes in v5:
time: 68.7 us; the launch traced here: 68.6 us
  blocking collectives  59.2 us (86%)
  Pallas kernels  5.49 us (8%)
  waiting for transfers between devices  2.76 us (4%)
  local copies, waits for them, and re-layouts  0.78 us (1%)
    all_to_all x2, blocking collectives, exchange(): lax.all_to_all(array.reshape(experts, PIECES, width), 'ep', split_axis=0,...  59.2 us
    pallas_call x7, Pallas kernels, call(): pl.pallas_call(kernel, out_shape=out_shape, in_specs=[VMEM] * len(args),...  5.49 us
    ppermute x1, waiting for transfers between devices, shards(): other = lax.ppermute(arrived, 'ep', partner)  1.45 us
  transfers between devices with their start and end apart: 2, of which 2 were waited for; matrix products, arithmetic and copies ran while one was open for 0% of the time, Pallas kernels for 1%

profile of v5, /device:TPU:514, one launch (start us, length us, event | category | flops | bytes accessed | tf_op | source)
XLA Modules:
  0.0 68.6 jit_solution(4716668006221737636)
XLA Ops:
  0.0 0.0 copy-start
  0.0 0.0 copy-start.2
  0.0 0.0 copy-start.1
  0.0 0.0 slice-start
  0.0 0.0 slice-start.2
  0.0 0.0 slice-start.4
  0.1 0.7 %copy-done = bf16[8,2880]{1,0:T(8,128)(2,1)S(1)} copy-done((bf16[8,2880]{1,0:T(8,128)(2,1)S(1)}, bf16[8,2880]{1,0:T(8,128)(2,1)}, u32[]{:S(2)}) %copy-start) | copy-done | bytes 46104
  0.8 0.0 copy-done.2
  0.8 0.0 copy-done.1
  0.8 0.0 copy-start.3
  0.8 0.0 slice-start.1
  0.8 0.0 slice-start.3
  0.8 0.0 slice-start.5
  0.8 0.4 route.1
  1.2 36.6 %all_to_all.10 = bf16[64,8,384]{2,1,0:T(8,128)(2,1)S(1)} all-to-all(bf16[64,8,384]{2,1,0:T(8,128)(2,1)S(1)} %bitcast.26), channel_id=1, replica_groups={{0,2,4,6,72,74,76,78,16,18,20,22,88,90,92,94,32,34,36,38,104,106,108,11..., dimensions={0} | all-to-all | bytes 786432 | tf_op jit(solution)/shard_map/all_to_all | solution.py:195
  37.8 0.0 collective-permute-start
  37.8 0.0 copy-done.3
  37.8 0.3 tables.1
  38.1 1.4 %collective-permute-done.other_ref = bf16[512,384]{1,0:T(8,128)(2,1)S(1)} collective-permute-done((bf16[512,384]{1,0:T(8,128)(2,1)S(1)}, bf16[512,384]{1,0:T(8,128)(2,1)S(1)}, u32[]{:S(2)}, u32[]{:S(2)}) %collective-permute-start) | collective-permute-done | bytes 393248 | tf_op jit(solution)/shard_map/ppermute | solution.py:221
  39.5 0.0 slice-done
  39.5 0.0 slice-done.2
  39.5 0.0 slice-done.4
  39.5 0.0 slice-done.1
  39.5 0.0 slice-done.3
  39.5 0.0 slice-done.5
  39.6 3.4 %expert.1 = (bf16[64,2880]{1,0:T(8,128)(2,1)S(1)}, bf16[64,2880]{1,0:T(8,128)(2,1)S(1)}) custom-call(bf16[64,2880]{1,0:T(8,128)(2,1)S(1)} %get-tuple-element.12.own_rows, bf16[512,384]{1,0:T(8,128)(2,1)S(1)} %collective-permute-done.other_ref, bf16[720,2880]{1,0:T(8,128)(2,1)S(1)} %bitcast.15, bf16[720,2880]{1,0:T(8,128)(2,1)S(1)} %bitcast.18, ...), custom_call_target="tpu_custom_call" | custom-call | flops 2000000000 | tf_op jit(solution)/shard_map/expert/pallas_call | solution.py:168
  43.0 0.3 collective-permute-start.1
  43.2 0.2 messages.1.own_ref
  43.5 1.3 %collective-permute-done.1.arrived_ref = bf16[64,2880]{1,0:T(8,128)(2,1)S(1)} collective-permute-done((bf16[64,2880]{1,0:T(8,128)(2,1)S(1)}, bf16[64,2880]{1,0:T(8,128)(2,1)S(1)}, u32[]{:S(2)}, u32[]{:S(2)}) %collective-permute-start.1) | collective-permute-done | bytes 368672 | tf_op jit(solution)/shard_map/ppermute | solution.py:242
  44.8 0.2 add.1
  45.1 22.6 %all_to_all.11 = bf16[64,8,384]{2,1,0:T(8,128)(2,1)S(1)} all-to-all(bf16[64,8,384]{2,1,0:T(8,128)(2,1)S(1)} %bitcast.23), channel_id=1, replica_groups={{0,2,4,6,72,74,76,78,16,18,20,22,88,90,92,94,32,34,36,38,104,106,108,11..., dimensions={0} | all-to-all | bytes 786432 | tf_op jit(solution)/shard_map/all_to_all | solution.py:195
  67.7 0.9 %combine.1 = bf16[8,2880]{1,0:T(8,128)(2,1)} custom-call(bf16[8,2880]{1,0:T(8,128)(2,1)S(1)} %copy-done, bf16[256,512]{1,0:T(8,128)(2,1)S(1)} %get-tuple-element.10.taking, f32[256,128]{1,0:T(8,128)S(1)} %get-tuple-element.11.weighing, bf16[512,384]{1,0:T(8,128)(2,1)S(1)} %bitcast.22), custom_call_target="tpu_custom_call" | custom-call | flops 1000000 | tf_op jit(solution)/shard_map/combine/pallas_call | solution.py:168
  (4 shorter events, 0.0 us)
Async XLA Ops:
  0.0 0.8 %copy-start = (bf16[8,2880]{1,0:T(8,128)(2,1)S(1)}, bf16[8,2880]{1,0:T(8,128)(2,1)}, u32[]{:S(2)}) copy-start(bf16[8,2880]{1,0:T(8,128)(2,1)} %tokens_ref.3) | copy-start | bytes 138244
  0.0 0.8 %copy-start.2 = (s32[8,4]{0,1:T(4,128)S(1)}, s32[8,4]{0,1:T(4,128)}, u32[]{:S(2)}) copy-start(s32[8,4]{0,1:T(4,128)} %param.9) | copy-start | bytes 388
  0.0 0.8 %copy-start.1 = (f32[2880]{0:T(1024)S(1)}, f32[2880]{0:T(1024)}, u32[]{:S(2)}) copy-start(f32[2880]{0:T(1024)} %gain_ref.1) | copy-start | bytes 34564
  0.0 39.5 %slice-start = ((s8[4239360]{0:T(1024)(128)(4,1)}), s8[4194304]{0:T(1024)(128)(4,1)S(1)}, s32[]{:S(2)}) async-start(s8[4239360]{0:T(1024)(128)(4,1)} %bitcast.13), calls=%async_computation.2 | async-start | bytes 8388608
  0.0 39.5 %slice-start.2 = ((s8[4239360]{0:T(1024)(128)(4,1)}), s8[4194304]{0:T(1024)(128)(4,1)S(1)}, s32[]{:S(2)}) async-start(s8[4239360]{0:T(1024)(128)(4,1)} %bitcast.16), calls=%async_computation.4 | async-start | bytes 8388608
  0.0 39.5 %slice-start.4 = ((s8[4239360]{0:T(1024)(128)(4,1)}), s8[4194304]{0:T(1024)(128)(4,1)S(1)}, s32[]{:S(2)}) async-start(s8[4239360]{0:T(1024)(128)(4,1)} %bitcast.19), calls=%async_computation.6 | async-start | bytes 8388608
  0.8 37.0 %copy-start.3 = (s32[8,4]{0,1:T(4,128)S(1)}, s32[8,4]{0,1:T(4,128)}, u32[]{:S(2)}) copy-start(s32[8,4]{0,1:T(4,128)} %param.10) | copy-start | bytes 388
  0.8 38.7 %slice-start.1 = ((s8[4239360]{0:T(1024)(128)(4,1)}), s8[45056]{0:T(1024)(128)(4,1)S(1)}, s32[]{:S(2)}) async-start(s8[4239360]{0:T(1024)(128)(4,1)} %bitcast.13), calls=%async_computation.3 | async-start | bytes 90112
  0.8 38.7 %slice-start.3 = ((s8[4239360]{0:T(1024)(128)(4,1)}), s8[45056]{0:T(1024)(128)(4,1)S(1)}, s32[]{:S(2)}) async-start(s8[4239360]{0:T(1024)(128)(4,1)} %bitcast.16), calls=%async_computation.5 | async-start | bytes 90112
  0.8 38.7 %slice-start.5 = ((s8[4239360]{0:T(1024)(128)(4,1)}), s8[45056]{0:T(1024)(128)(4,1)S(1)}, s32[]{:S(2)}) async-start(s8[4239360]{0:T(1024)(128)(4,1)} %bitcast.19), calls=%async_computation.7 | async-start | bytes 90112
  37.8 1.7 %collective-permute-start = (bf16[512,384]{1,0:T(8,128)(2,1)S(1)}, bf16[512,384]{1,0:T(8,128)(2,1)S(1)}, u32[]{:S(2)}, u32[]{:S(2)}) collective-permute-start(bf16[512,384]{1,0:T(8,128)(2,1)S(1)} %bitcast.24), channel_id=1, source_target_pairs={{0,1},{1,0},{2,3},{3,2},{4,5},{5,4},{6,7},{7,6},{8,9},{9,8},{10,11... | collective-permute-start | bytes 1179656 | tf_op jit(solution)/shard_map/ppermute | solution.py:221
  43.0 1.8 %collective-permute-start.1 = (bf16[64,2880]{1,0:T(8,128)(2,1)S(1)}, bf16[64,2880]{1,0:T(8,128)(2,1)S(1)}, u32[]{:S(2)}, u32[]{:S(2)}) collective-permute-start(bf16[64,2880]{1,0:T(8,128)(2,1)S(1)} %get-tuple-element.14), channel_id=1, source_target_pairs={{0,1},{1,0},{2,3},{3,2},{4,5},{5,4},{6,7},{7,6},{8,9},{9,8},{10,11... | collective-permute-start | bytes 1105928 | tf_op jit(solution)/shard_map/ppermute | solution.py:242

commit v6 on v5

--- a/solution.py
+++ b/solution.py
@@ -118,9 +118,13 @@
 def expert_kernel(own_rows, other_ref, gate_ref, up_ref, down_ref, own_out, other_out):
     rows, model = own_rows.shape
     x = jnp.concatenate([own_rows[...], rows_of(other_ref)[:, :model]], axis=0)
-    gate = lax.dot_general(gate_ref[...], x, NT, preferred_element_type=F32)
-    up = lax.dot_general(up_ref[...], x, NT, preferred_element_type=F32)
-    hidden = (gate * jax.nn.sigmoid(gate) * up).T.astype(BF16)
+    cut = gate_ref.shape[0] // 256 * 128 + 128
+    parts = []
+    for low, high in ((0, cut), (cut, gate_ref.shape[0])):
+        gate = lax.dot_general(gate_ref[low:high], x, NT, preferred_element_type=F32)
+        up = lax.dot_general(up_ref[low:high], x, NT, preferred_element_type=F32)
+        parts.append((gate * jax.nn.sigmoid(gate) * up).astype(BF16).T)
+    hidden = jnp.concatenate(parts, axis=1)
     out = matmul(hidden, down_ref[...]).astype(BF16)
     own_out[...] = out[:rows]
     other_out[...] = out[rows:]

time: 68.7 us -> 68.7 us (level)
  no operation moved by 1% of the time
where the time goes in v6:
time: 68.7 us; the launch traced here: 68.6 us
  blocking collectives  59.2 us (86%)
  Pallas kernels  5.48 us (8%)
  waiting for transfers between devices  2.76 us (4%)
  local copies, waits for them, and re-layouts  0.78 us (1%)
    all_to_all x2, blocking collectives, exchange(): lax.all_to_all(array.reshape(experts, PIECES, width), 'ep', split_axis=0,...  59.2 us
    pallas_call x7, Pallas kernels, call(): pl.pallas_call(kernel, out_shape=out_shape, in_specs=[VMEM] * len(args),...  5.48 us
    ppermute x1, waiting for transfers between devices, shards(): other = lax.ppermute(arrived, 'ep', partner)  1.45 us
  transfers between devices with their start and end apart: 2, of which 2 were waited for; matrix products, arithmetic and copies ran while one was open for 0% of the time, Pallas kernels for 1%

profile of v6, /device:TPU:514, one launch (start us, length us, event | category | flops | bytes accessed | tf_op | source)
XLA Modules:
  0.0 68.6 jit_solution(10208402122873443025)
XLA Ops:
  0.0 0.0 copy-start
  0.0 0.0 copy-start.2
  0.0 0.0 copy-start.1
  0.0 0.0 slice-start
  0.0 0.0 slice-start.2
  0.0 0.0 slice-start.4
  0.1 0.7 %copy-done = bf16[8,2880]{1,0:T(8,128)(2,1)S(1)} copy-done((bf16[8,2880]{1,0:T(8,128)(2,1)S(1)}, bf16[8,2880]{1,0:T(8,128)(2,1)}, u32[]{:S(2)}) %copy-start) | copy-done | bytes 46104
  0.8 0.0 copy-done.2
  0.8 0.0 copy-done.1
  0.8 0.0 copy-start.3
  0.8 0.0 slice-start.1
  0.8 0.0 slice-start.3
  0.8 0.0 slice-start.5
  0.8 0.4 route.1
  1.2 36.6 %all_to_all.10 = bf16[64,8,384]{2,1,0:T(8,128)(2,1)S(1)} all-to-all(bf16[64,8,384]{2,1,0:T(8,128)(2,1)S(1)} %bitcast.26), channel_id=1, replica_groups={{0,2,4,6,72,74,76,78,16,18,20,22,88,90,92,94,32,34,36,38,104,106,108,11..., dimensions={0} | all-to-all | bytes 786432 | tf_op jit(solution)/shard_map/all_to_all | solution.py:199
  37.8 0.0 collective-permute-start
  37.8 0.0 copy-done.3
  37.8 0.3 tables.1
  38.1 1.4 %collective-permute-done.other_ref = bf16[512,384]{1,0:T(8,128)(2,1)S(1)} collective-permute-done((bf16[512,384]{1,0:T(8,128)(2,1)S(1)}, bf16[512,384]{1,0:T(8,128)(2,1)S(1)}, u32[]{:S(2)}, u32[]{:S(2)}) %collective-permute-start) | collective-permute-done | bytes 393248 | tf_op jit(solution)/shard_map/ppermute | solution.py:225
  39.5 0.0 slice-done
  39.5 0.0 slice-done.2
  39.5 0.0 slice-done.4
  39.5 0.0 slice-done.1
  39.5 0.0 slice-done.3
  39.5 0.0 slice-done.5
  39.6 3.4 %expert.1 = (bf16[64,2880]{1,0:T(8,128)(2,1)S(1)}, bf16[64,2880]{1,0:T(8,128)(2,1)S(1)}) custom-call(bf16[64,2880]{1,0:T(8,128)(2,1)S(1)} %get-tuple-element.12.own_rows, bf16[512,384]{1,0:T(8,128)(2,1)S(1)} %collective-permute-done.other_ref, bf16[720,2880]{1,0:T(8,128)(2,1)S(1)} %bitcast.15, bf16[720,2880]{1,0:T(8,128)(2,1)S(1)} %bitcast.18, ...), custom_call_target="tpu_custom_call" | custom-call | flops 2000000000 | tf_op jit(solution)/shard_map/expert/pallas_call | solution.py:172
  43.0 0.2 collective-permute-start.1
  43.2 0.3 messages.1.own_ref
  43.5 1.3 %collective-permute-done.1.arrived_ref = bf16[64,2880]{1,0:T(8,128)(2,1)S(1)} collective-permute-done((bf16[64,2880]{1,0:T(8,128)(2,1)S(1)}, bf16[64,2880]{1,0:T(8,128)(2,1)S(1)}, u32[]{:S(2)}, u32[]{:S(2)}) %collective-permute-start.1) | collective-permute-done | bytes 368672 | tf_op jit(solution)/shard_map/ppermute | solution.py:246
  44.8 0.2 add.1
  45.0 22.6 %all_to_all.11 = bf16[64,8,384]{2,1,0:T(8,128)(2,1)S(1)} all-to-all(bf16[64,8,384]{2,1,0:T(8,128)(2,1)S(1)} %bitcast.23), channel_id=1, replica_groups={{0,2,4,6,72,74,76,78,16,18,20,22,88,90,92,94,32,34,36,38,104,106,108,11..., dimensions={0} | all-to-all | bytes 786432 | tf_op jit(solution)/shard_map/all_to_all | solution.py:199
  67.7 0.9 %combine.1 = bf16[8,2880]{1,0:T(8,128)(2,1)} custom-call(bf16[8,2880]{1,0:T(8,128)(2,1)S(1)} %copy-done, bf16[256,512]{1,0:T(8,128)(2,1)S(1)} %get-tuple-element.10.taking, f32[256,128]{1,0:T(8,128)S(1)} %get-tuple-element.11.weighing, bf16[512,384]{1,0:T(8,128)(2,1)S(1)} %bitcast.22), custom_call_target="tpu_custom_call" | custom-call | flops 1000000 | tf_op jit(solution)/shard_map/combine/pallas_call | solution.py:172
  (4 shorter events, 0.0 us)
Async XLA Ops:
  0.0 0.8 %copy-start = (bf16[8,2880]{1,0:T(8,128)(2,1)S(1)}, bf16[8,2880]{1,0:T(8,128)(2,1)}, u32[]{:S(2)}) copy-start(bf16[8,2880]{1,0:T(8,128)(2,1)} %tokens_ref.3) | copy-start | bytes 138244
  0.0 0.8 %copy-start.2 = (s32[8,4]{0,1:T(4,128)S(1)}, s32[8,4]{0,1:T(4,128)}, u32[]{:S(2)}) copy-start(s32[8,4]{0,1:T(4,128)} %param.9) | copy-start | bytes 388
  0.0 0.8 %copy-start.1 = (f32[2880]{0:T(1024)S(1)}, f32[2880]{0:T(1024)}, u32[]{:S(2)}) copy-start(f32[2880]{0:T(1024)} %gain_ref.1) | copy-start | bytes 34564
  0.0 39.5 %slice-start = ((s8[4239360]{0:T(1024)(128)(4,1)}), s8[4194304]{0:T(1024)(128)(4,1)S(1)}, s32[]{:S(2)}) async-start(s8[4239360]{0:T(1024)(128)(4,1)} %bitcast.13), calls=%async_computation.2 | async-start | bytes 8388608
  0.0 39.5 %slice-start.2 = ((s8[4239360]{0:T(1024)(128)(4,1)}), s8[4194304]{0:T(1024)(128)(4,1)S(1)}, s32[]{:S(2)}) async-start(s8[4239360]{0:T(1024)(128)(4,1)} %bitcast.16), calls=%async_computation.4 | async-start | bytes 8388608
  0.0 39.5 %slice-start.4 = ((s8[4239360]{0:T(1024)(128)(4,1)}), s8[4194304]{0:T(1024)(128)(4,1)S(1)}, s32[]{:S(2)}) async-start(s8[4239360]{0:T(1024)(128)(4,1)} %bitcast.19), calls=%async_computation.6 | async-start | bytes 8388608
  0.8 37.0 %copy-start.3 = (s32[8,4]{0,1:T(4,128)S(1)}, s32[8,4]{0,1:T(4,128)}, u32[]{:S(2)}) copy-start(s32[8,4]{0,1:T(4,128)} %param.10) | copy-start | bytes 388
  0.8 38.7 %slice-start.1 = ((s8[4239360]{0:T(1024)(128)(4,1)}), s8[45056]{0:T(1024)(128)(4,1)S(1)}, s32[]{:S(2)}) async-start(s8[4239360]{0:T(1024)(128)(4,1)} %bitcast.13), calls=%async_computation.3 | async-start | bytes 90112
  0.8 38.7 %slice-start.3 = ((s8[4239360]{0:T(1024)(128)(4,1)}), s8[45056]{0:T(1024)(128)(4,1)S(1)}, s32[]{:S(2)}) async-start(s8[4239360]{0:T(1024)(128)(4,1)} %bitcast.16), calls=%async_computation.5 | async-start | bytes 90112
  0.8 38.7 %slice-start.5 = ((s8[4239360]{0:T(1024)(128)(4,1)}), s8[45056]{0:T(1024)(128)(4,1)S(1)}, s32[]{:S(2)}) async-start(s8[4239360]{0:T(1024)(128)(4,1)} %bitcast.19), calls=%async_computation.7 | async-start | bytes 90112
  37.8 1.7 %collective-permute-start = (bf16[512,384]{1,0:T(8,128)(2,1)S(1)}, bf16[512,384]{1,0:T(8,128)(2,1)S(1)}, u32[]{:S(2)}, u32[]{:S(2)}) collective-permute-start(bf16[512,384]{1,0:T(8,128)(2,1)S(1)} %bitcast.24), channel_id=1, source_target_pairs={{0,1},{1,0},{2,3},{3,2},{4,5},{5,4},{6,7},{7,6},{8,9},{9,8},{10,11... | collective-permute-start | bytes 1179656 | tf_op jit(solution)/shard_map/ppermute | solution.py:225
  43.0 1.8 %collective-permute-start.1 = (bf16[64,2880]{1,0:T(8,128)(2,1)S(1)}, bf16[64,2880]{1,0:T(8,128)(2,1)S(1)}, u32[]{:S(2)}, u32[]{:S(2)}) collective-permute-start(bf16[64,2880]{1,0:T(8,128)(2,1)S(1)} %get-tuple-element.14), channel_id=1, source_target_pairs={{0,1},{1,0},{2,3},{3,2},{4,5},{5,4},{6,7},{7,6},{8,9},{9,8},{10,11... | collective-permute-start | bytes 1105928 | tf_op jit(solution)/shard_map/ppermute | solution.py:246

commit v7 on v6

--- a/solution.py
+++ b/solution.py
@@ -118,9 +118,10 @@
 def expert_kernel(own_rows, other_ref, gate_ref, up_ref, down_ref, own_out, other_out):
     rows, model = own_rows.shape
     x = jnp.concatenate([own_rows[...], rows_of(other_ref)[:, :model]], axis=0)
-    cut = gate_ref.shape[0] // 256 * 128 + 128
+    units = gate_ref.shape[0]
     parts = []
-    for low, high in ((0, cut), (cut, gate_ref.shape[0])):
+    for low in range(0, units, 256):
+        high = min(low + 256, units)
         gate = lax.dot_general(gate_ref[low:high], x, NT, preferred_element_type=F32)
         up = lax.dot_general(up_ref[low:high], x, NT, preferred_element_type=F32)
         parts.append((gate * jax.nn.sigmoid(gate) * up).astype(BF16).T)

time: 68.7 us -> 68.7 us (level)
  no operation moved by 1% of the time
where the time goes in v7:
time: 68.7 us; the launch traced here: 68.6 us
  blocking collectives  59.2 us (86%)
  Pallas kernels  5.45 us (8%)
  waiting for transfers between devices  2.76 us (4%)
  local copies, waits for them, and re-layouts  0.78 us (1%)
    all_to_all x2, blocking collectives, exchange(): lax.all_to_all(array.reshape(experts, PIECES, width), 'ep', split_axis=0,...  59.2 us
    pallas_call x7, Pallas kernels, call(): pl.pallas_call(kernel, out_shape=out_shape, in_specs=[VMEM] * len(args),...  5.45 us
    ppermute x1, waiting for transfers between devices, shards(): other = lax.ppermute(arrived, 'ep', partner)  1.45 us
  transfers between devices with their start and end apart: 2, of which 2 were waited for; matrix products, arithmetic and copies ran while one was open for 0% of the time, Pallas kernels for 1%

profile of v7, /device:TPU:514, one launch (start us, length us, event | category | flops | bytes accessed | tf_op | source)
XLA Modules:
  0.0 68.6 jit_solution(10702236465658559310)
XLA Ops:
  0.0 0.0 copy-start
  0.0 0.0 copy-start.2
  0.0 0.0 copy-start.1
  0.0 0.0 slice-start
  0.0 0.0 slice-start.2
  0.0 0.0 slice-start.4
  0.1 0.7 %copy-done = bf16[8,2880]{1,0:T(8,128)(2,1)S(1)} copy-done((bf16[8,2880]{1,0:T(8,128)(2,1)S(1)}, bf16[8,2880]{1,0:T(8,128)(2,1)}, u32[]{:S(2)}) %copy-start) | copy-done | bytes 46104
  0.8 0.0 copy-done.2
  0.8 0.0 copy-done.1
  0.8 0.0 copy-start.3
  0.8 0.0 slice-start.1
  0.8 0.0 slice-start.3
  0.8 0.0 slice-start.5
  0.8 0.4 route.1
  1.2 36.6 %all_to_all.10 = bf16[64,8,384]{2,1,0:T(8,128)(2,1)S(1)} all-to-all(bf16[64,8,384]{2,1,0:T(8,128)(2,1)S(1)} %bitcast.26), channel_id=1, replica_groups={{0,2,4,6,72,74,76,78,16,18,20,22,88,90,92,94,32,34,36,38,104,106,108,11..., dimensions={0} | all-to-all | bytes 786432 | tf_op jit(solution)/shard_map/all_to_all | solution.py:200
  37.8 0.0 collective-permute-start
  37.8 0.0 copy-done.3
  37.8 0.3 tables.1
  38.1 1.4 %collective-permute-done.other_ref = bf16[512,384]{1,0:T(8,128)(2,1)S(1)} collective-permute-done((bf16[512,384]{1,0:T(8,128)(2,1)S(1)}, bf16[512,384]{1,0:T(8,128)(2,1)S(1)}, u32[]{:S(2)}, u32[]{:S(2)}) %collective-permute-start) | collective-permute-done | bytes 393248 | tf_op jit(solution)/shard_map/ppermute | solution.py:226
  39.5 0.0 slice-done
  39.5 0.0 slice-done.2
  39.5 0.0 slice-done.4
  39.5 0.0 slice-done.1
  39.5 0.0 slice-done.3
  39.5 0.0 slice-done.5
  39.6 3.4 %expert.1 = (bf16[64,2880]{1,0:T(8,128)(2,1)S(1)}, bf16[64,2880]{1,0:T(8,128)(2,1)S(1)}) custom-call(bf16[64,2880]{1,0:T(8,128)(2,1)S(1)} %get-tuple-element.12.own_rows, bf16[512,384]{1,0:T(8,128)(2,1)S(1)} %collective-permute-done.other_ref, bf16[720,2880]{1,0:T(8,128)(2,1)S(1)} %bitcast.15, bf16[720,2880]{1,0:T(8,128)(2,1)S(1)} %bitcast.18, ...), custom_call_target="tpu_custom_call" | custom-call | flops 2000000000 | tf_op jit(solution)/shard_map/expert/pallas_call | solution.py:173
  42.9 0.2 collective-permute-start.1
  43.2 0.3 messages.1.own_ref
  43.5 1.3 %collective-permute-done.1.arrived_ref = bf16[64,2880]{1,0:T(8,128)(2,1)S(1)} collective-permute-done((bf16[64,2880]{1,0:T(8,128)(2,1)S(1)}, bf16[64,2880]{1,0:T(8,128)(2,1)S(1)}, u32[]{:S(2)}, u32[]{:S(2)}) %collective-permute-start.1) | collective-permute-done | bytes 368672 | tf_op jit(solution)/shard_map/ppermute | solution.py:247
  44.8 0.2 add.1
  45.0 22.6 %all_to_all.11 = bf16[64,8,384]{2,1,0:T(8,128)(2,1)S(1)} all-to-all(bf16[64,8,384]{2,1,0:T(8,128)(2,1)S(1)} %bitcast.23), channel_id=1, replica_groups={{0,2,4,6,72,74,76,78,16,18,20,22,88,90,92,94,32,34,36,38,104,106,108,11..., dimensions={0} | all-to-all | bytes 786432 | tf_op jit(solution)/shard_map/all_to_all | solution.py:200
  67.6 0.9 %combine.1 = bf16[8,2880]{1,0:T(8,128)(2,1)} custom-call(bf16[8,2880]{1,0:T(8,128)(2,1)S(1)} %copy-done, bf16[256,512]{1,0:T(8,128)(2,1)S(1)} %get-tuple-element.10.taking, f32[256,128]{1,0:T(8,128)S(1)} %get-tuple-element.11.weighing, bf16[512,384]{1,0:T(8,128)(2,1)S(1)} %bitcast.22), custom_call_target="tpu_custom_call" | custom-call | flops 1000000 | tf_op jit(solution)/shard_map/combine/pallas_call | solution.py:173
  (4 shorter events, 0.0 us)
Async XLA Ops:
  0.0 0.8 %copy-start = (bf16[8,2880]{1,0:T(8,128)(2,1)S(1)}, bf16[8,2880]{1,0:T(8,128)(2,1)}, u32[]{:S(2)}) copy-start(bf16[8,2880]{1,0:T(8,128)(2,1)} %tokens_ref.3) | copy-start | bytes 138244
  0.0 0.8 %copy-start.2 = (s32[8,4]{0,1:T(4,128)S(1)}, s32[8,4]{0,1:T(4,128)}, u32[]{:S(2)}) copy-start(s32[8,4]{0,1:T(4,128)} %param.9) | copy-start | bytes 388
  0.0 0.8 %copy-start.1 = (f32[2880]{0:T(1024)S(1)}, f32[2880]{0:T(1024)}, u32[]{:S(2)}) copy-start(f32[2880]{0:T(1024)} %gain_ref.1) | copy-start | bytes 34564
  0.0 39.5 %slice-start = ((s8[4239360]{0:T(1024)(128)(4,1)}), s8[4194304]{0:T(1024)(128)(4,1)S(1)}, s32[]{:S(2)}) async-start(s8[4239360]{0:T(1024)(128)(4,1)} %bitcast.13), calls=%async_computation.2 | async-start | bytes 8388608
  0.0 39.5 %slice-start.2 = ((s8[4239360]{0:T(1024)(128)(4,1)}), s8[4194304]{0:T(1024)(128)(4,1)S(1)}, s32[]{:S(2)}) async-start(s8[4239360]{0:T(1024)(128)(4,1)} %bitcast.16), calls=%async_computation.4 | async-start | bytes 8388608
  0.0 39.5 %slice-start.4 = ((s8[4239360]{0:T(1024)(128)(4,1)}), s8[4194304]{0:T(1024)(128)(4,1)S(1)}, s32[]{:S(2)}) async-start(s8[4239360]{0:T(1024)(128)(4,1)} %bitcast.19), calls=%async_computation.6 | async-start | bytes 8388608
  0.8 37.0 %copy-start.3 = (s32[8,4]{0,1:T(4,128)S(1)}, s32[8,4]{0,1:T(4,128)}, u32[]{:S(2)}) copy-start(s32[8,4]{0,1:T(4,128)} %param.10) | copy-start | bytes 388
  0.8 38.7 %slice-start.1 = ((s8[4239360]{0:T(1024)(128)(4,1)}), s8[45056]{0:T(1024)(128)(4,1)S(1)}, s32[]{:S(2)}) async-start(s8[4239360]{0:T(1024)(128)(4,1)} %bitcast.13), calls=%async_computation.3 | async-start | bytes 90112
  0.8 38.7 %slice-start.3 = ((s8[4239360]{0:T(1024)(128)(4,1)}), s8[45056]{0:T(1024)(128)(4,1)S(1)}, s32[]{:S(2)}) async-start(s8[4239360]{0:T(1024)(128)(4,1)} %bitcast.16), calls=%async_computation.5 | async-start | bytes 90112
  0.8 38.7 %slice-start.5 = ((s8[4239360]{0:T(1024)(128)(4,1)}), s8[45056]{0:T(1024)(128)(4,1)S(1)}, s32[]{:S(2)}) async-start(s8[4239360]{0:T(1024)(128)(4,1)} %bitcast.19), calls=%async_computation.7 | async-start | bytes 90112
  37.8 1.7 %collective-permute-start = (bf16[512,384]{1,0:T(8,128)(2,1)S(1)}, bf16[512,384]{1,0:T(8,128)(2,1)S(1)}, u32[]{:S(2)}, u32[]{:S(2)}) collective-permute-start(bf16[512,384]{1,0:T(8,128)(2,1)S(1)} %bitcast.24), channel_id=1, source_target_pairs={{0,1},{1,0},{2,3},{3,2},{4,5},{5,4},{6,7},{7,6},{8,9},{9,8},{10,11... | collective-permute-start | bytes 1179656 | tf_op jit(solution)/shard_map/ppermute | solution.py:226
  42.9 1.8 %collective-permute-start.1 = (bf16[64,2880]{1,0:T(8,128)(2,1)S(1)}, bf16[64,2880]{1,0:T(8,128)(2,1)S(1)}, u32[]{:S(2)}, u32[]{:S(2)}) collective-permute-start(bf16[64,2880]{1,0:T(8,128)(2,1)S(1)} %get-tuple-element.14), channel_id=1, source_target_pairs={{0,1},{1,0},{2,3},{3,2},{4,5},{5,4},{6,7},{7,6},{8,9},{9,8},{10,11... | collective-permute-start | bytes 1105928 | tf_op jit(solution)/shard_map/ppermute | solution.py:247

commit v8 on v7

--- a/solution.py
+++ b/solution.py
@@ -75,18 +75,14 @@
     return matmul(swap_matrix(BLOCK, PIECES), stack_pieces(rows, width))
 
 
-def spread_kernel(spread_ref):
-    count, columns = spread_ref.shape
-    spread_ref[...] = onehot(iota((count, columns), 1) % count == iota((count, columns), 0))
-
-
-def route_kernel(tokens_ref, gain_ref, ids_ref, spread_ref, out_ref, *, experts, width):
-    top, count = ids_ref.shape
-    columns = PIECES * count
-    piece = iota((top, columns), 1) // count
-    row = iota((experts * PIECES, columns), 0)
-    ids = ids_ref[...].astype(F32).astype(BF16)
-    wanted = place(matmul(ids, spread_ref[...]).astype(jnp.int32), experts) * PIECES + piece
+def slots_kernel(slots_ref, *, count):
+    slots_ref[...] = iota(slots_ref.shape, 0) - iota(slots_ref.shape, 1) // count
+
+
+def route_kernel(tokens_ref, gain_ref, ids_ref, slots_ref, out_ref, *, experts, width):
+    top = ids_ref.shape[0]
+    row = slots_ref[...]
+    wanted = jnp.concatenate([place(ids_ref[...], experts) * PIECES] * PIECES, axis=1)
     hit = row == wanted[0:1, :]
     for k in range(1, top):
         hit = jnp.logical_or(hit, row == wanted[k : k + 1, :])
@@ -206,18 +202,18 @@
             tiled=True,
         ).reshape(slots, width)
 
-    spread = call(
-        spread_kernel,
-        jax.ShapeDtypeStruct((count, PIECES * count), BF16),
+    table = call(
+        functools.partial(slots_kernel, count=count),
+        jax.ShapeDtypeStruct((slots, PIECES * count), jnp.int32),
         (),
-        name="spread",
+        name="slots",
         mib=1,
         flops=5_000_000_000,
     )
     outgoing = call(
         functools.partial(route_kernel, experts=experts, width=width),
         message,
-        (tokens, norm_gain, ids, spread),
+        (tokens, norm_gain, ids, table),
         name="route",
         mib=4,
         flops=20_000_000_000,

time: 68.7 us -> 68.7 us (level)
  no operation moved by 1% of the time
where the time goes in v8:
time: 68.7 us; the launch traced here: 68.5 us
  blocking collectives  59.2 us (86%)
  Pallas kernels  5.44 us (8%)
  waiting for transfers between devices  2.75 us (4%)
  local copies, waits for them, and re-layouts  0.76 us (1%)
    all_to_all x2, blocking collectives, exchange(): lax.all_to_all(array.reshape(experts, PIECES, width), 'ep', split_axis=0,...  59.2 us
    pallas_call x7, Pallas kernels, call(): pl.pallas_call(kernel, out_shape=out_shape, in_specs=[VMEM] * len(args),...  5.44 us
    ppermute x1, waiting for transfers between devices, shards(): other = lax.ppermute(arrived, 'ep', partner)  1.45 us
  transfers between devices with their start and end apart: 2, of which 2 were waited for; matrix products, arithmetic and copies ran while one was open for 0% of the time, Pallas kernels for 1%

profile of v8, /device:TPU:514, one launch (start us, length us, event | category | flops | bytes accessed | tf_op | source)
XLA Modules:
  0.0 68.5 jit_solution(2189470673612713420)
XLA Ops:
  0.0 0.0 copy-start
  0.0 0.0 copy-start.2
  0.0 0.0 copy-start.1
  0.0 0.0 slice-start
  0.1 0.0 slice-start.2
  0.1 0.0 slice-start.4
  0.1 0.7 %copy-done = bf16[8,2880]{1,0:T(8,128)(2,1)S(1)} copy-done((bf16[8,2880]{1,0:T(8,128)(2,1)S(1)}, bf16[8,2880]{1,0:T(8,128)(2,1)}, u32[]{:S(2)}) %copy-start) | copy-done | bytes 46104
  0.8 0.0 copy-done.2
  0.8 0.0 copy-done.1
  0.8 0.0 copy-start.3
  0.8 0.0 slice-start.1
  0.8 0.0 slice-start.3
  0.8 0.0 slice-start.5
  0.8 0.4 route.1
  1.2 36.6 %all_to_all.10 = bf16[64,8,384]{2,1,0:T(8,128)(2,1)S(1)} all-to-all(bf16[64,8,384]{2,1,0:T(8,128)(2,1)S(1)} %bitcast.26), channel_id=1, replica_groups={{0,2,4,6,72,74,76,78,16,18,20,22,88,90,92,94,32,34,36,38,104,106,108,11..., dimensions={0} | all-to-all | bytes 786432 | tf_op jit(solution)/shard_map/all_to_all | solution.py:196
  37.8 0.0 collective-permute-start
  37.8 0.0 copy-done.3
  37.8 0.3 tables.1
  38.0 1.4 %collective-permute-done.other_ref = bf16[512,384]{1,0:T(8,128)(2,1)S(1)} collective-permute-done((bf16[512,384]{1,0:T(8,128)(2,1)S(1)}, bf16[512,384]{1,0:T(8,128)(2,1)S(1)}, u32[]{:S(2)}, u32[]{:S(2)}) %collective-permute-start) | collective-permute-done | bytes 393248 | tf_op jit(solution)/shard_map/ppermute | solution.py:222
  39.5 0.0 slice-done
  39.5 0.0 slice-done.2
  39.5 0.0 slice-done.4
  39.5 0.0 slice-done.1
  39.5 0.0 slice-done.3
  39.5 0.0 slice-done.5
  39.6 3.4 %expert.1 = (bf16[64,2880]{1,0:T(8,128)(2,1)S(1)}, bf16[64,2880]{1,0:T(8,128)(2,1)S(1)}) custom-call(bf16[64,2880]{1,0:T(8,128)(2,1)S(1)} %get-tuple-element.12.own_rows, bf16[512,384]{1,0:T(8,128)(2,1)S(1)} %collective-permute-done.other_ref, bf16[720,2880]{1,0:T(8,128)(2,1)S(1)} %bitcast.15, bf16[720,2880]{1,0:T(8,128)(2,1)S(1)} %bitcast.18, ...), custom_call_target="tpu_custom_call" | custom-call | flops 2000000000 | tf_op jit(solution)/shard_map/expert/pallas_call | solution.py:169
  42.9 0.3 collective-permute-start.1
  43.2 0.3 messages.1.own_ref
  43.4 1.3 %collective-permute-done.1.arrived_ref = bf16[64,2880]{1,0:T(8,128)(2,1)S(1)} collective-permute-done((bf16[64,2880]{1,0:T(8,128)(2,1)S(1)}, bf16[64,2880]{1,0:T(8,128)(2,1)S(1)}, u32[]{:S(2)}, u32[]{:S(2)}) %collective-permute-start.1) | collective-permute-done | bytes 368672 | tf_op jit(solution)/shard_map/ppermute | solution.py:243
  44.7 0.2 add.1
  45.0 22.6 %all_to_all.11 = bf16[64,8,384]{2,1,0:T(8,128)(2,1)S(1)} all-to-all(bf16[64,8,384]{2,1,0:T(8,128)(2,1)S(1)} %bitcast.23), channel_id=1, replica_groups={{0,2,4,6,72,74,76,78,16,18,20,22,88,90,92,94,32,34,36,38,104,106,108,11..., dimensions={0} | all-to-all | bytes 786432 | tf_op jit(solution)/shard_map/all_to_all | solution.py:196
  67.6 0.9 %combine.1 = bf16[8,2880]{1,0:T(8,128)(2,1)} custom-call(bf16[8,2880]{1,0:T(8,128)(2,1)S(1)} %copy-done, bf16[256,512]{1,0:T(8,128)(2,1)S(1)} %get-tuple-element.10.taking, f32[256,128]{1,0:T(8,128)S(1)} %get-tuple-element.11.weighing, bf16[512,384]{1,0:T(8,128)(2,1)S(1)} %bitcast.22), custom_call_target="tpu_custom_call" | custom-call | flops 1000000 | tf_op jit(solution)/shard_map/combine/pallas_call | solution.py:169
  (4 shorter events, 0.0 us)
Async XLA Ops:
  0.0 0.8 %copy-start = (bf16[8,2880]{1,0:T(8,128)(2,1)S(1)}, bf16[8,2880]{1,0:T(8,128)(2,1)}, u32[]{:S(2)}) copy-start(bf16[8,2880]{1,0:T(8,128)(2,1)} %tokens_ref.3) | copy-start | bytes 138244
  0.0 0.8 %copy-start.2 = (s32[8,4]{0,1:T(4,128)S(1)}, s32[8,4]{0,1:T(4,128)}, u32[]{:S(2)}) copy-start(s32[8,4]{0,1:T(4,128)} %param.9) | copy-start | bytes 388
  0.0 0.8 %copy-start.1 = (f32[2880]{0:T(1024)S(1)}, f32[2880]{0:T(1024)}, u32[]{:S(2)}) copy-start(f32[2880]{0:T(1024)} %gain_ref.1) | copy-start | bytes 34564
  0.0 39.4 %slice-start = ((s8[4239360]{0:T(1024)(128)(4,1)}), s8[4194304]{0:T(1024)(128)(4,1)S(1)}, s32[]{:S(2)}) async-start(s8[4239360]{0:T(1024)(128)(4,1)} %bitcast.13), calls=%async_computation.2 | async-start | bytes 8388608
  0.1 39.4 %slice-start.2 = ((s8[4239360]{0:T(1024)(128)(4,1)}), s8[4194304]{0:T(1024)(128)(4,1)S(1)}, s32[]{:S(2)}) async-start(s8[4239360]{0:T(1024)(128)(4,1)} %bitcast.16), calls=%async_computation.4 | async-start | bytes 8388608
  0.1 39.4 %slice-start.4 = ((s8[4239360]{0:T(1024)(128)(4,1)}), s8[4194304]{0:T(1024)(128)(4,1)S(1)}, s32[]{:S(2)}) async-start(s8[4239360]{0:T(1024)(128)(4,1)} %bitcast.19), calls=%async_computation.6 | async-start | bytes 8388608
  0.8 37.0 %copy-start.3 = (s32[8,4]{0,1:T(4,128)S(1)}, s32[8,4]{0,1:T(4,128)}, u32[]{:S(2)}) copy-start(s32[8,4]{0,1:T(4,128)} %param.10) | copy-start | bytes 388
  0.8 38.7 %slice-start.1 = ((s8[4239360]{0:T(1024)(128)(4,1)}), s8[45056]{0:T(1024)(128)(4,1)S(1)}, s32[]{:S(2)}) async-start(s8[4239360]{0:T(1024)(128)(4,1)} %bitcast.13), calls=%async_computation.3 | async-start | bytes 90112
  0.8 38.7 %slice-start.3 = ((s8[4239360]{0:T(1024)(128)(4,1)}), s8[45056]{0:T(1024)(128)(4,1)S(1)}, s32[]{:S(2)}) async-start(s8[4239360]{0:T(1024)(128)(4,1)} %bitcast.16), calls=%async_computation.5 | async-start | bytes 90112
  0.8 38.7 %slice-start.5 = ((s8[4239360]{0:T(1024)(128)(4,1)}), s8[45056]{0:T(1024)(128)(4,1)S(1)}, s32[]{:S(2)}) async-start(s8[4239360]{0:T(1024)(128)(4,1)} %bitcast.19), calls=%async_computation.7 | async-start | bytes 90112
  37.8 1.7 %collective-permute-start = (bf16[512,384]{1,0:T(8,128)(2,1)S(1)}, bf16[512,384]{1,0:T(8,128)(2,1)S(1)}, u32[]{:S(2)}, u32[]{:S(2)}) collective-permute-start(bf16[512,384]{1,0:T(8,128)(2,1)S(1)} %bitcast.24), channel_id=1, source_target_pairs={{0,1},{1,0},{2,3},{3,2},{4,5},{5,4},{6,7},{7,6},{8,9},{9,8},{10,11... | collective-permute-start | bytes 1179656 | tf_op jit(solution)/shard_map/ppermute | solution.py:222
  42.9 1.8 %collective-permute-start.1 = (bf16[64,2880]{1,0:T(8,128)(2,1)S(1)}, bf16[64,2880]{1,0:T(8,128)(2,1)S(1)}, u32[]{:S(2)}, u32[]{:S(2)}) collective-permute-start(bf16[64,2880]{1,0:T(8,128)(2,1)S(1)} %get-tuple-element.14), channel_id=1, source_target_pairs={{0,1},{1,0},{2,3},{3,2},{4,5},{5,4},{6,7},{7,6},{8,9},{9,8},{10,11... | collective-permute-start | bytes 1105928 | tf_op jit(solution)/shard_map/ppermute | solution.py:243
